TPU v7x, 256 devices: a whole 4x4x8 slice. The times are simulated.
256 devices in a mesh: chan: 16 (over z_hi, y, core), prof: 16 (over z_lo, x).
Axes of the slice: x: 4, y: 4, z: 8 (z_hi: 2, z_lo: 4; z = z_hi * 4 + z_lo), core: 2. Of those that a mesh axis runs over, the one named last changes fastest.
Arguments:
- observed: bfloat16 [256, 8448], P('prof', 'chan'), may hold values from -6 to 6
- eigvec: bfloat16 [8448, 300], P('chan'), may hold values from -0.0625 to 0.0625
- jacobian: bfloat16 [256, 8448, 400], P('prof', 'chan'), may hold values from -0.44921875 to 0.44921875
- radiance_base: bfloat16 [8448], P('chan'), may hold values from -1 to 1
- curvature: bfloat16 [8448], P('chan'), may hold values from -0.29882812 to 0.29882812
- block_mask: int32 [256, 256], P('prof', 'chan'), may hold values 0 or 1
- pc_weight: float32 [300], replicated, may hold values from 0.2 to 2
- prior_prec: float32 [400], replicated, may hold values from 0.3 to 3
- prior_mean: float32 [256, 400], P(('prof', 'chan')), may hold values from -6 to 6
- state0: float32 [256, 400], P(('prof', 'chan')), may hold values from -6 to 6
Outputs:
- states: float32 [256, 400], P(('prof', 'chan'))
All inputs are finite; a program needn't handle non-finite values. No bound on the sum of `block_mask` on one device may be relied on, other than what follows from the above.
Results may differ from a plain program's by a relative error of at most 0.006.
Values may be sent and summed in bfloat16 or wider, within the bound.
No kernel may reach another device: no remote copies, remote signals or barrier semaphores. Data moves between devices by JAX's collectives and lax.ppermute only.
A program may use at most 128 MiB of HBM per device.

v0:
```python
import jax
import jax.numpy as jnp
from jax import lax
from jax.sharding import PartitionSpec as P

ITERS = 2


def laid_out(parts, dim):
    lengths = list(parts.shape[1:])
    lengths[dim] *= parts.shape[0]
    return jnp.moveaxis(parts, 0, dim).reshape(lengths)


def copy_for_each(value, axis):
    copies = jnp.broadcast_to(value, (lax.axis_size(axis), *value.shape))
    return lax.all_to_all(copies, axis, split_axis=0, concat_axis=0, tiled=True)


def gathered_copies(value, axis, dim):
    return laid_out(copy_for_each(value, axis), dim)


def solve_step(states, pc_resid, pc_jacob, pc_weight, prior_prec, prior_mean):
    highest = lax.Precision.HIGHEST
    weighted_jac = pc_jacob * pc_weight[None, :, None]
    normal = jnp.einsum("rks,rkt->rst", weighted_jac, pc_jacob, precision=highest)
    normal = (
        normal + jnp.eye(pc_jacob.shape[2], dtype=jnp.float32)[None] * prior_prec[None, None, :]
    )
    gradient = jnp.einsum("rks,rk->rs", pc_jacob, pc_weight[None, :] * pc_resid, precision=highest)
    gradient = gradient + prior_prec[None, :] * (states - prior_mean)
    factor = jnp.linalg.cholesky(normal)

    def one_solve(fac, vec):
        return jax.scipy.linalg.cho_solve((fac, True), vec)

    update = jax.vmap(one_solve)(factor, gradient)
    return states - update


def project(state_bf, spectra, valid, eigvec, jacobian, radiance_base, curvature):
    shift_f = radiance_base.astype(jnp.float32)
    curve_f = curvature.astype(jnp.float32)
    linear = jnp.einsum("rs,rcs->rc", state_bf, jacobian, preferred_element_type=jnp.float32)
    misfit = (
        valid * (shift_f + linear + 0.5 * curve_f * linear * linear - spectra.astype(jnp.float32))
    ).astype(jnp.bfloat16)
    slope = valid * (1.0 + curve_f * linear)
    weighted = (slope[:, :, None] * eigvec[None]).astype(jnp.bfloat16)
    pc_resid = jnp.dot(misfit, eigvec, preferred_element_type=jnp.float32)
    pc_jacob = jnp.einsum("rck,rcs->rks", weighted, jacobian, preferred_element_type=jnp.float32)
    return (pc_resid, pc_jacob)


def local(
    observed,
    eigvec,
    jacobian,
    radiance_base,
    curvature,
    block_mask,
    pc_weight,
    prior_prec,
    prior_mean,
    state0,
):
    block_width = observed.shape[1] // block_mask.shape[1]
    states = state0
    valid = jnp.repeat(block_mask.astype(jnp.float32), block_width, axis=1)
    for iteration in range(ITERS):
        state_bf = gathered_copies(states.astype(jnp.bfloat16), "chan", 0)
        pc_resid, pc_jacob = project(
            state_bf, observed, valid, eigvec, jacobian, radiance_base, curvature
        )
        pc_resid, pc_jacob = (
            lax.psum_scatter(pc_resid, "chan", scatter_dimension=0, tiled=True),
            lax.psum_scatter(pc_jacob, "chan", scatter_dimension=0, tiled=True),
        )
        states = solve_step(states, pc_resid, pc_jacob, pc_weight, prior_prec, prior_mean)
    return states


def solution(mesh):
    return jax.shard_map(
        local,
        mesh=mesh,
        in_specs=(
            P("prof", "chan"),
            P("chan", None),
            P("prof", "chan", None),
            P("chan"),
            P("chan"),
            P("prof", "chan"),
            P(),
            P(),
            P(("prof", "chan"), None),
            P(("prof", "chan"), None),
        ),
        out_specs=P(("prof", "chan"), None),
        check_vma=False,
    )
```

profile of v0, /device:TPU:2, one launch (start us, length us, event | category | flops | bytes accessed | tf_op | source)
XLA Modules:
  0.0 635.0 jit_solution(3634729615285331142)
XLA Ops:
  7.9 0.8 reduce.32
  9.3 11.2 %all-to-all-start = ((bf16[16,2,200]{2,1,0:T(2,128)(2,1)}), bf16[16,2,200]{2,1,0:T(2,128)(2,1)S(1)}, u32[]{:S(2)}, u32[]{:S(2)}) async-start(bf16[16,2,200]{2,1,0:T(2,128)(2,1)} %reshape.526), calls=%async_computation | async-start | bytes 32768 | tf_op jit(solution)/shard_map/all_to_all | solution.py:17
  20.6 0.7 convert_element_type.44
  22.2 1.0 convert_element_type.48
  23.2 7.3 %all-to-all-done = bf16[16,2,200]{2,1,0:T(2,128)(2,1)S(1)} async-done(((bf16[16,2,200]{2,1,0:T(2,128)(2,1)}), bf16[16,2,200]{2,1,0:T(2,128)(2,1)S(1)}, u32[]{:S(2)}, u32[]{:S(2)}) %all-to-all-start) | async-done | bytes 12832 | tf_op jit(solution)/shard_map/all_to_all | solution.py:17
  30.6 4.7 fusion.82
  35.4 0.9 copy-done
  36.3 7.7 %fusion = f32[16,300,400]{1,2,0:T(8,128)} fusion(bf16[16,528,400]{1,2,0:T(8,128)(2,1)S(1)} %copy-done, f32[528,300]{0,1:T(8,128)S(1)} %convert_element_type.48, f32[16,528]{1,0:T(8,128)S(1)} %fusion.79), kind=kOutput, calls=%fused_computation.6 | convolution fusion | flops 2032588800 | bytes 15105792 | tf_op jit(solution)/shard_map/rck,rcs->rks/dot_general | solution.py:52
  46.8 103.9 %all-reduce.3 = f32[16,300]{1,0:T(8,128)} all-reduce(f32[16,300]{1,0:T(8,128)S(1)} %fusion.86), channel_id=3, replica_groups=mesh['chan'=16,'prof'=16] {'chan'}, use_global_device_ids=true, to_apply=%region_9.11.clone | all-reduce | flops 4800 | bytes 38400
  150.7 43.0 %reduce-scatter.3.cloned.1.call-done = f32[1,300,400]{1,2,0:T(8,128)} async-done(((f32[16,300,400]{1,2,0:T(8,128)}), f32[1,300,400]{1,2,0:T(8,128)}) %reduce-scatter.3.cloned.1.call-update) | async-done | bytes 480016 | tf_op jit(solution)/shard_map/reduce_scatter | solution.py:78
  193.7 2.8 convolution_add_fusion.1
  197.0 11.7 %custom-call.37 = f32[1,128,128]{2,1,0:T(8,128)S(1)} custom-call(f32[1,128,128]{2,1,0:T(8,128)S(1)} %cholesky.439), custom_call_target="Cholesky" | custom-call | tf_op jit(solution)/shard_map/jit(cholesky)/cholesky | solution.py:33
  208.8 9.8 %custom-call.38 = f32[1,1,128,128]{2,3,1,0:T(8,128)S(1)} custom-call(f32[1,1,128,128]{3,2,1,0:T(8,128)S(1)} %get-tuple-element.60), custom_call_target="InvertDiagBlocksLowerTriangular" | custom-call | tf_op jit(solution)/shard_map/jit(cholesky)/cholesky | solution.py:33
  219.3 12.1 %custom-call.39 = f32[1,128,128]{2,1,0:T(8,128)S(1)} custom-call(f32[1,128,128]{2,1,0:T(8,128)S(1)} %cholesky.443), custom_call_target="Cholesky" | custom-call | tf_op jit(solution)/shard_map/jit(cholesky)/cholesky | solution.py:33
  231.4 9.8 %custom-call.40 = f32[1,1,128,128]{2,3,1,0:T(8,128)S(1)} custom-call(f32[1,1,128,128]{3,2,1,0:T(8,128)S(1)} %get-tuple-element.57), custom_call_target="InvertDiagBlocksLowerTriangular" | custom-call | tf_op jit(solution)/shard_map/jit(cholesky)/cholesky | solution.py:33
  241.8 11.7 %custom-call.41 = f32[1,128,128]{2,1,0:T(8,128)S(1)} custom-call(f32[1,128,128]{2,1,0:T(8,128)S(1)} %cholesky.448), custom_call_target="Cholesky" | custom-call | tf_op jit(solution)/shard_map/jit(cholesky)/cholesky | solution.py:33
  253.5 0.7 compare_reduce_fusion.5
  254.2 9.8 %custom-call.42 = f32[1,1,128,128]{2,3,1,0:T(8,128)S(1)} custom-call(f32[1,1,128,128]{3,2,1,0:T(8,128)S(1)} %get-tuple-element.54), custom_call_target="InvertDiagBlocksLowerTriangular" | custom-call | tf_op jit(solution)/shard_map/jit(cholesky)/cholesky | solution.py:33
  264.4 1.5 custom-call.43
  266.5 0.7 compare_reduce_fusion.6
  270.5 6.1 while.4
  271.2 1.3 bitcast_dynamic-update-slice_fusion.4
  273.3 1.3 bitcast_dynamic-update-slice_fusion.4
  275.3 1.3 bitcast_dynamic-update-slice_fusion.4
  276.6 0.9 fusion.57
  277.6 39.3 %custom-call.44 = f32[1,4,128,128]{2,3,1,0:T(8,128)S(1)} custom-call(f32[1,4,128,128]{3,2,1,0:T(8,128)S(1)} %pad_maximum_fusion), custom_call_target="InvertDiagBlocksLowerTriangular" | custom-call | tf_op jit(solution)/shard_map/vmap(jit(_cho_solve))/triangular_solve | solution.py:36
  317.0 2.0 fusion.17
  321.6 0.8 reduce.33
  322.5 13.6 %all_to_all.10 = bf16[16,2,200]{2,1,0:T(2,128)(2,1)S(1)} all-to-all(bf16[16,2,200]{2,1,0:T(2,128)(2,1)S(1)} %reshape.528), channel_id=1, replica_groups=mesh['chan'=16,'prof'=16] {'chan'}, dimensions={0} | all-to-all | bytes 25600 | tf_op jit(solution)/shard_map/all_to_all | solution.py:17
  336.2 4.6 fusion.80
  340.8 10.8 %fusion.1 = f32[16,300,400]{1,2,0:T(8,128)} fusion(bf16[16,528,400]{1,2,0:T(8,128)(2,1)} %param.15, f32[16,528]{1,0:T(8,128)S(1)} %fusion.77, f32[528,300]{0,1:T(8,128)S(1)} %copy-done.5), kind=kOutput, calls=%fused_computation.7 | convolution fusion | flops 2032588800 | bytes 15105792 | tf_op jit(solution)/shard_map/rck,rcs->rks/dot_general | solution.py:52
  351.9 90.3 %all-reduce.4 = f32[16,300]{1,0:T(8,128)S(1)} all-reduce(f32[16,300]{1,0:T(8,128)S(1)} %fusion.84), channel_id=5, replica_groups=mesh['chan'=16,'prof'=16] {'chan'}, use_global_device_ids=true, to_apply=%region_11.14.clone | all-reduce | flops 4800 | bytes 38400
  442.2 59.5 %reduce-scatter.5.cloned.1.call-done = f32[1,300,400]{1,2,0:T(8,128)} async-done(((f32[16,300,400]{1,2,0:T(8,128)}), f32[1,300,400]{1,2,0:T(8,128)}) %reduce-scatter.5.cloned.1.call-update) | async-done | bytes 480016 | tf_op jit(solution)/shard_map/reduce_scatter | solution.py:78
  501.7 2.8 convolution_add_fusion
  505.0 11.7 %custom-call.45 = f32[1,128,128]{2,1,0:T(8,128)S(1)} custom-call(f32[1,128,128]{2,1,0:T(8,128)S(1)} %cholesky.452), custom_call_target="Cholesky" | custom-call | tf_op jit(solution)/shard_map/jit(cholesky)/cholesky | solution.py:33
  516.8 9.8 %custom-call.46 = f32[1,1,128,128]{2,3,1,0:T(8,128)S(1)} custom-call(f32[1,1,128,128]{3,2,1,0:T(8,128)S(1)} %get-tuple-element.52), custom_call_target="InvertDiagBlocksLowerTriangular" | custom-call | tf_op jit(solution)/shard_map/jit(cholesky)/cholesky | solution.py:33
  527.2 11.9 %custom-call.47 = f32[1,128,128]{2,1,0:T(8,128)S(1)} custom-call(f32[1,128,128]{2,1,0:T(8,128)S(1)} %cholesky.456), custom_call_target="Cholesky" | custom-call | tf_op jit(solution)/shard_map/jit(cholesky)/cholesky | solution.py:33
  540.5 9.8 %custom-call.48 = f32[1,1,128,128]{2,3,1,0:T(8,128)S(1)} custom-call(f32[1,1,128,128]{3,2,1,0:T(8,128)S(1)} %get-tuple-element.49), custom_call_target="InvertDiagBlocksLowerTriangular" | custom-call | tf_op jit(solution)/shard_map/jit(cholesky)/cholesky | solution.py:33
  550.8 11.7 %custom-call.49 = f32[1,128,128]{2,1,0:T(8,128)S(1)} custom-call(f32[1,128,128]{2,1,0:T(8,128)S(1)} %cholesky.461), custom_call_target="Cholesky" | custom-call | tf_op jit(solution)/shard_map/jit(cholesky)/cholesky | solution.py:33
  563.2 9.8 %custom-call.50 = f32[1,1,128,128]{2,3,1,0:T(8,128)S(1)} custom-call(f32[1,1,128,128]{3,2,1,0:T(8,128)S(1)} %get-tuple-element.46), custom_call_target="InvertDiagBlocksLowerTriangular" | custom-call | tf_op jit(solution)/shard_map/jit(cholesky)/cholesky | solution.py:33
  573.4 1.5 custom-call.51
  574.9 0.7 compare_reduce_fusion
  578.2 5.7 while.5
  578.8 1.3 bitcast_dynamic-update-slice_fusion.5
  580.8 1.3 bitcast_dynamic-update-slice_fusion.5
  582.7 1.3 bitcast_dynamic-update-slice_fusion.5
  584.1 39.3 %custom-call.52 = f32[1,4,128,128]{2,3,1,0:T(8,128)S(1)} custom-call(f32[1,4,128,128]{3,2,1,0:T(8,128)S(1)} %pad_maximum_fusion.1), custom_call_target="InvertDiagBlocksLowerTriangular" | custom-call | tf_op jit(solution)/shard_map/vmap(jit(_cho_solve))/triangular_solve | solution.py:36
  623.4 1.3 fusion.16
  (143 shorter events, 23.7 us)
Async XLA Ops:
  9.3 21.2 %all-to-all-start = ((bf16[16,2,200]{2,1,0:T(2,128)(2,1)}), bf16[16,2,200]{2,1,0:T(2,128)(2,1)S(1)}, u32[]{:S(2)}, u32[]{:S(2)}) async-start(bf16[16,2,200]{2,1,0:T(2,128)(2,1)} %reshape.526), calls=%async_computation | async-start | bytes 32768 | tf_op jit(solution)/shard_map/all_to_all | solution.py:17
  20.5 173.1 %reduce-scatter.3.cloned.1.call-start = ((), (), s32[]{:S(2)}) async-start(), calls=%async_computation.4 | async-start | bytes 10444800 | tf_op jit(solution)/shard_map/reduce_scatter | solution.py:78
  23.2 20.7 %copy-start.4 = (f32[528,300]{0,1:T(8,128)}, f32[528,300]{0,1:T(8,128)S(1)}, u32[]{:S(2)}) copy-start(f32[528,300]{0,1:T(8,128)S(1)} %convert_element_type.48) | copy-start | bytes 1900804
  30.6 5.7 copy-start
  44.0 0.7 copy-start.13
  44.0 0.7 copy-start.10
  44.0 0.7 copy-start.14
  44.0 2.6 copy-start.12
  44.0 2.5 copy-start.3
  44.0 2.5 copy-start.7
  44.0 149.7 %copy-start.8 = (f32[400]{0:T(512)S(1)}, f32[400]{0:T(512)}, u32[]{:S(2)}) copy-start(f32[400]{0:T(512)} %param.20) | copy-start | bytes 4804
  44.1 272.9 %copy-start.9 = (f32[1,400]{1,0:T(1,128)S(1)}, f32[1,400]{1,0:T(1,128)}, u32[]{:S(2)}) copy-start(f32[1,400]{1,0:T(1,128)} %param.22) | copy-start | bytes 4804
  44.1 272.9 %copy-start.11 = (f32[1,400]{1,0:T(1,128)S(1)}, f32[1,400]{1,0:T(1,128)}, u32[]{:S(2)}) copy-start(f32[1,400]{1,0:T(1,128)} %param.21) | copy-start | bytes 4804
  44.1 457.6 %reduce-scatter.5.cloned.1.call-start = ((), (), s32[]{:S(2)}) async-start(), calls=%async_computation.5 | async-start | bytes 10444800 | tf_op jit(solution)/shard_map/reduce_scatter | solution.py:78
  193.7 123.3 %copy-start.1 = (f32[1,300,400]{1,2,0:T(8,128)S(1)}, f32[1,300,400]{1,2,0:T(8,128)}, u32[]{:S(2)}) copy-start(f32[1,300,400]{1,2,0:T(8,128)} %reduce-scatter.3.cloned.1.call-done) | copy-start | bytes 1440004
  270.5 70.3 %copy-start.5 = (f32[528,300]{0,1:T(8,128)S(1)}, f32[528,300]{0,1:T(8,128)}, u32[]{:S(2)}) copy-start(f32[528,300]{0,1:T(8,128)} %copy-done.4) | copy-start | bytes 1900804
  351.7 232.3 %copy-start.6 = (f32[1,128,112]{2,1,0:T(8,128)S(1)}, f32[1,128,112]{2,1,0:T(8,128)}, u32[]{:S(2)}) copy-start(f32[1,128,112]{2,1,0:T(8,128)} %convert_bitcast_fusion) | copy-start | bytes 172036
  501.7 121.7 %copy-start.2 = (f32[1,300,400]{1,2,0:T(8,128)S(1)}, f32[1,300,400]{1,2,0:T(8,128)}, u32[]{:S(2)}) copy-start(f32[1,300,400]{1,2,0:T(8,128)} %reduce-scatter.5.cloned.1.call-done) | copy-start | bytes 1440004
Sparse Core Ops, SparseCore 0:
  44.2 149.4 reduce-scatter.2
  351.8 149.8 reduce-scatter.4
where the time goes:
time: 639 us; the launch traced here: 635 us
  other arithmetic  224 us (35%)
  blocking collectives  208 us (33%)
  waiting for transfers between devices  110 us (17%)
  matrix products  45 us (7%)
  between operations  19.3 us (3%)
  local copies, waits for them, and re-layouts  17.2 us (3%)
  starting transfers between devices  11.3 us (2%)
    unnamed x2, blocking collectives  194 us
    another operation x29, other arithmetic, solve_step(): factor = jnp.linalg.cholesky(normal)  138 us
    reduce_scatter x2, waiting for transfers between devices, local(): lax.psum_scatter(pc_jacob, 'chan', scatter_dimension=0, tiled=True)  103 us
    another operation x11, other arithmetic, one_solve(): return jax.scipy.linalg.cho_solve((fac, True), vec)  81.1 us
    dot_general x2, matrix products, project(): jnp.einsum('rck,rcs->rks', weighted, jacobian, preferred_element_type=jnp...  18.5 us
    all_to_all x1, blocking collectives, copy_for_each(): return lax.all_to_all(copies, axis, split_axis=0, concat_axis=0, tiled=True)  13.6 us
  transfers between devices with their start and end apart: 3, of which 3 were waited for; matrix products, arithmetic and copies ran while one was open for 1% of the time, Pallas kernels for 0%

commit v1 on v0

v1 whole, which is shorter than its diff:
```python
import functools

import jax
import jax.numpy as jnp
from jax import lax
from jax.experimental import pallas as pl
from jax.experimental.pallas import tpu as pltpu
from jax.sharding import PartitionSpec as P

ITERS = 2
HIGHEST = lax.Precision.HIGHEST
f32, bf16 = jnp.float32, jnp.bfloat16

ROWS = 304
TOP = 128
LOW = ROWS - TOP
CUT = 3 * TOP + 16
FOLD = CUT + 3 * LOW
BLOCK = FOLD + 32
GRANT = pltpu.CompilerParams(vmem_limit_bytes=14 * 2**20)


def dot_nn(a, b, precision=HIGHEST):
    dims = (((1,), (0,)), ((), ()))
    return lax.dot_general(a, b, dims, precision=precision, preferred_element_type=f32)


def dot_nt(a, b, precision=HIGHEST):
    dims = (((1,), (1,)), ((), ()))
    return lax.dot_general(a, b, dims, precision=precision, preferred_element_type=f32)


def owner_of(dy, dz, dc):
    me = lax.axis_index("chan")
    z, y, core = lax.div(me, 8), lax.rem(lax.div(me, 2), 4), lax.rem(me, 2)
    return lax.rem(z + dz, 2) * 8 + lax.rem(y + dy, 4) * 2 + lax.rem(core + dc, 2)


def mask_kernel(mask_ref, valid_ref):
    blocks, width = mask_ref.shape[1], valid_ref.shape[1]
    owner = lax.broadcasted_iota(jnp.int32, (blocks, width), 0) * (width // blocks)
    channel = lax.broadcasted_iota(jnp.int32, (blocks, width), 1)
    spread = jnp.where((channel >= owner) & (channel < owner + width // blocks), 1.0, 0.0)
    valid_ref[...] = dot_nn(mask_ref[...].astype(f32).astype(bf16), spread.astype(bf16), None)


def valid_channels(block_mask, width):
    return pl.pallas_call(
        mask_kernel,
        out_shape=jax.ShapeDtypeStruct((block_mask.shape[0], width), f32),
        cost_estimate=pl.CostEstimate(flops=2 * 10**10, bytes_accessed=0, transcendentals=0),
        compiler_params=GRANT,
        name="valid_channels",
    )(block_mask)


def slope_kernel(*refs):
    fours, refs = refs[:4], refs[4:]
    observed_ref, valid_ref, base_ref, curve_ref, eig_ref, jac_ref = refs[:6]
    slope_ref, resid_ref, linear_ref = refs[6:]
    profiles, width = observed_ref.shape
    valid = valid_ref[...]
    state = jnp.concatenate([ref[...].astype(f32) for ref in fours], axis=0).astype(bf16)
    for slot in range(profiles):
        p = owner_of(slot // 4, slot // 2 % 2, slot % 2)
        linear_ref[pl.ds(p, 1), :] = dot_nn(state, jac_ref[p], None)[slot : slot + 1]
    linear = linear_ref[...]
    base = base_ref[...].astype(f32).reshape(1, width)
    curve = curve_ref[...].astype(f32).reshape(1, width)
    misfit = valid * (
        base + linear + 0.5 * curve * linear * linear - observed_ref[...].astype(f32)
    )
    slope_ref[...] = valid * (1.0 + curve * linear)
    resid = dot_nt(misfit.astype(bf16), eig_ref[...], None)
    resid_ref[...] = jnp.pad(resid, ((0, 0), (0, 384 - resid.shape[1])))


def slopes(fours, observed, valid, base, curve, eig_t, jac_t):
    profiles, states, width = jac_t.shape
    vmem = pl.BlockSpec(memory_space=pltpu.VMEM)
    return pl.pallas_call(
        slope_kernel,
        out_shape=(
            jax.ShapeDtypeStruct((profiles, width), f32),
            jax.ShapeDtypeStruct((profiles, 384), f32),
        ),
        in_specs=[vmem] * 10,
        out_specs=(vmem, vmem),
        scratch_shapes=[pltpu.VMEM((profiles, width), f32)],
        cost_estimate=pl.CostEstimate(flops=10**9, bytes_accessed=0, transcendentals=0),
        compiler_params=GRANT,
        name="slopes",
    )(*fours, observed, valid, base, curve, eig_t, jac_t)


def project_kernel(dy, slope_ref, resid_ref, eig_ref, jac_ref, keep_ref, send_ref):
    states = jac_ref.shape[1]

    def folded(part, group):
        part = jnp.pad(part, ((0, 8 * group - part.shape[0]), (0, 512 - states)))
        total = part[0:group]
        for i in range(1, 8):
            total += pltpu.roll(part[group * i : group * i + group], 16 * i, 1)
        return total

    def one(dz, dc, out_ref):
        p = owner_of(dy, dz, dc)
        weighted = (slope_ref[pl.ds(p, 1), :] * eig_ref[...].astype(f32)).astype(bf16)
        pc = dot_nt(weighted, jac_ref[p], None)
        pc = jnp.pad(pc, ((0, ROWS - pc.shape[0]), (0, 0)))
        for i in range(3):
            tile = pc[:, i * 128 : (i + 1) * 128]
            out_ref[dz, i * TOP : (i + 1) * TOP, :] = tile[:TOP]
            out_ref[dz, CUT + i * LOW : CUT + (i + 1) * LOW, :] = tile[TOP:]
        out_ref[dz, 3 * TOP : CUT, :] = folded(pc[:TOP, 384:states], 16)
        out_ref[dz, FOLD : FOLD + 24, :] = folded(pc[TOP:, 384:states], 24)
        resid = resid_ref[pl.ds(p, 1), :]
        high = resid.astype(bf16).astype(f32)
        low = resid - high
        rows = [part[:, 128 * i : 128 * i + 128] for part in (high, low) for i in range(3)]
        rows.append(jnp.zeros((2, 128), f32))
        out_ref[dz, FOLD + 24 : BLOCK, :] = jnp.concatenate(rows, axis=0)

    def step(dz, carry):
        one(dz, 1, send_ref)
        one(dz, 0, keep_ref)
        return carry

    lax.fori_loop(0, 2, step, 0)


def project(dy, slope, resid, eig_t, jac_t):
    vmem = pl.BlockSpec(memory_space=pltpu.VMEM)
    shape = (2, BLOCK, 128)
    return pl.pallas_call(
        functools.partial(project_kernel, dy),
        out_shape=(jax.ShapeDtypeStruct(shape, f32),) * 2,
        in_specs=[vmem] * 4,
        out_specs=(vmem, vmem),
        cost_estimate=pl.CostEstimate(flops=10**9, bytes_accessed=0, transcendentals=0),
        compiler_params=GRANT,
        name="project",
    )(slope, resid, eig_t, jac_t)


def spread_lane(tile, j):
    return jnp.broadcast_to(tile[:, j : j + 1], (8, 128))


def spread_row(tile, j):
    return jnp.broadcast_to(tile[j : j + 1, :], (8, 128))


def spd_inverse(tiles):
    sub = lax.broadcasted_iota(jnp.int32, (8, 128), 0)
    lane = lax.broadcasted_iota(jnp.int32, (8, 128), 1)
    count = len(tiles)
    units = [jnp.where(lane - 8 * i == sub, 1.0, 0.0) for i in range(count)]
    reduced = []
    cols = [spread_lane(tiles[0], j) for j in range(8)]
    for k in range(count):
        pivot, unit = tiles[k], units[k]
        follow = k + 1 < count
        ahead, coming, factors = [], [], []
        if follow:
            ahead = [spread_lane(tiles[k], 8 * k + 8 + j) for j in range(8)]
            coming = [spread_lane(tiles[k + 1], 8 * k + 8 + j) for j in range(8)]
            factors = [spread_lane(tiles[k + 1], 8 * k + j) for j in range(8)]
        diagonal = spread_row(cols[0], 0)
        scale = None
        for j in range(8):
            inverse = 1.0 / diagonal
            if j < 7:
                cross = cols[j] * spread_row(cols[j + 1], j)
                diagonal = spread_row(cols[j + 1], j + 1) - spread_row(cross, j + 1) * inverse
            scale = jnp.where(sub == j, inverse, scale) if j else inverse
            gain = jnp.where(sub == j, 0.0, cols[j] * inverse)

            def eliminated(value):
                return value - gain * spread_row(value, j)

            for m in range(j + 1, 8):
                cols[m] = eliminated(cols[m])
            pivot, unit = eliminated(pivot), eliminated(unit)
            ahead = [eliminated(value) for value in ahead]
        unit *= scale
        reduced.append(unit)
        if not follow:
            break
        pivot *= scale
        rows = [spread_row(pivot, j) for j in range(8)]
        unit_rows = [spread_row(unit, j) for j in range(8)]
        for i in range(k + 1, count):
            each = factors if i == k + 1 else [spread_lane(tiles[i], 8 * k + j) for j in range(8)]
            for j in range(8):
                tiles[i] = tiles[i] - each[j] * rows[j]
                units[i] = units[i] - each[j] * unit_rows[j]
        cols = []
        for value, start in zip(ahead, coming):
            value *= scale
            for m in range(8):
                start -= factors[m] * spread_row(value, m)
            cols.append(start)
    lower, scaled = jnp.concatenate(units, axis=0), jnp.concatenate(reduced, axis=0)
    dims = (((0,), (0,)), ((), ()))
    return lax.dot_general(lower, scaled, dims, precision=HIGHEST, preferred_element_type=f32)


def unfolded(block, rows, group):
    packed = block[3 * rows : 3 * rows + group]
    lane = lax.broadcasted_iota(jnp.int32, (group, 128), 1)
    last = [packed if i == 0 else pltpu.roll(packed, 128 - 16 * i, 1) for i in range(8)]
    last = jnp.concatenate([jnp.where(lane < 16, part, 0.0) for part in last], axis=0)
    tiles = [block[i * rows : (i + 1) * rows] for i in range(3)]
    return jnp.concatenate(tiles + [last[:rows]], axis=1)


def plus_diagonal(square, row):
    i0 = lax.broadcasted_iota(jnp.int32, square.shape, 0)
    i1 = lax.broadcasted_iota(jnp.int32, square.shape, 1)
    return square + jnp.where(i0 == i1, row, 0.0)


def tiles_of(square):
    return [square[i : i + 8] for i in range(0, square.shape[0], 8)]


def wide(row, size, fill=0.0):
    return jnp.pad(row, ((0, 0), (0, size - row.shape[1])), constant_values=fill)


def top_kernel(keep_ref, got_ref, prec_ref, weight_ref, jac_ref, inv_ref):
    block = keep_ref[...] + got_ref[...].astype(f32)
    jac = unfolded(block, TOP, 16) * wide(1.0 / jnp.sqrt(prec_ref[...]), 512)
    jac_ref[...] = jac
    s = plus_diagonal(dot_nt(jac, jac), 1.0 / weight_ref[...].reshape(1, -1)[:, :TOP])
    inv_ref[...] = spd_inverse(tiles_of(s))


def top_step(keep, got, prec, weight):
    return pl.pallas_call(
        top_kernel,
        out_shape=(
            jax.ShapeDtypeStruct((TOP, 512), f32),
            jax.ShapeDtypeStruct((TOP, TOP), f32),
        ),
        cost_estimate=pl.CostEstimate(flops=10**9, bytes_accessed=0, transcendentals=0),
        compiler_params=GRANT,
        name="top_step",
    )(keep, got, prec, weight)


def low_kernel(
    keep_ref, got_ref, top_ref, inv_ref, state_ref, prec_ref, mean_ref, weight_ref,
    out_ref, short_ref,
):
    block = keep_ref[...] + got_ref[...].astype(f32)
    root = jnp.sqrt(prec_ref[...])
    scale = wide(1.0 / root, 512)
    noise = wide(1.0 / weight_ref[...].reshape(1, -1)[:, TOP:], LOW, 1.0)
    low = unfolded(block, LOW, 24) * scale
    top, inv0 = top_ref[...], inv_ref[...]
    first = BLOCK - CUT - 8
    v = [block[first + i : first + i + 1] + block[first + 3 + i : first + 4 + i] for i in range(3)]
    v0 = jnp.broadcast_to(v[0], (8, 128))
    v12 = jnp.broadcast_to(jnp.concatenate(v[1:], axis=1)[:, :LOW], (8, LOW))
    shift = wide(root * (state_ref[...] - mean_ref[...]), 512)
    shift = jnp.broadcast_to(shift, (8, 512))
    v0 -= dot_nt(shift, top)
    v12 -= dot_nt(shift, low)
    s10 = dot_nt(low, top)
    t10 = dot_nn(s10, inv0)
    s = plus_diagonal(dot_nt(low, low), noise) - dot_nt(t10, s10)
    v12 -= dot_nt(v0, t10)
    inv1 = spd_inverse(tiles_of(s[:128, :128]))
    s21 = s[128:, :128]
    t21 = dot_nn(s21, inv1)
    s22 = s[128:, 128:] - dot_nt(t21, s21)
    s22 = jnp.pad(s22, ((0, 0), (0, 256 - LOW)))
    v1 = v12[:, :128]
    v2 = v12[:, 128:] - dot_nt(v1, t21)
    inv2 = spd_inverse(tiles_of(s22))[: LOW - 128]
    y2 = dot_nn(v2, inv2)[:, : LOW - 128]
    y1 = dot_nn(v1 - dot_nn(y2, s21), inv1)
    y12 = jnp.concatenate([y1, y2], axis=1)
    y0 = dot_nn(v0 - dot_nn(y12, s10), inv0)
    step = (dot_nn(y0, top) + dot_nn(y12, low)) * scale
    new = mean_ref[...] - step[0:1, : mean_ref.shape[1]]
    out_ref[...] = new
    short_ref[...] = new.astype(bf16)


def low_step(keep, got, top, inv0, state, prec, mean, weight):
    return pl.pallas_call(
        low_kernel,
        out_shape=(
            jax.ShapeDtypeStruct(mean.shape, f32),
            jax.ShapeDtypeStruct(mean.shape, bf16),
        ),
        cost_estimate=pl.CostEstimate(flops=10**9, bytes_accessed=0, transcendentals=0),
        compiler_params=GRANT,
        name="low_step",
    )(keep, got, top, inv0, state, prec, mean, weight)


def index_of(z, y, core):
    return z * 8 + y * 2 + core


MEMBERS = [(z, y, core) for z in range(2) for y in range(4) for core in range(2)]


def swap_core(value):
    return lax.ppermute(
        value, "chan", [(index_of(z, y, c), index_of(z, y, 1 - c)) for z, y, c in MEMBERS]
    )


def move_y(value, step):
    return lax.ppermute(
        value, "chan", [(index_of(z, y, c), index_of(z, (y + step) % 4, c)) for z, y, c in MEMBERS]
    )


def swap_z(value):
    return lax.ppermute(
        value, "chan", [(index_of(z, y, c), index_of(1 - z, y, c)) for z, y, c in MEMBERS]
    )


def gathered(value):
    pair = jnp.concatenate([value, swap_core(value)], axis=0)
    four = jnp.concatenate([pair, swap_z(pair)], axis=0)
    return [four] + [move_y(four, -dy) for dy in (1, 2, 3)]


def after(value, *others):
    return lax.optimization_barrier((value, *others))[0]


def local(
    observed, eigvec, jacobian, radiance_base, curvature, block_mask,
    pc_weight, prior_prec, prior_mean, state0,
):
    eig_t = eigvec.T
    jac_t = jnp.swapaxes(jacobian, 1, 2)
    prec = prior_prec.reshape(1, -1)

    def iterate(_, carry):
        state, short = carry
        fours = gathered(short)
        valid = valid_channels(after(block_mask, short), observed.shape[1])
        slope, resid = slopes(
            fours, observed, valid, radiance_base, curvature, eig_t, jac_t
        )

        def chip_sum(dy, here):
            keep, send = project(dy, here, resid, eig_t, jac_t)
            return keep, swap_core(send)

        def chunk(pair, part, dz):
            return pair[0][dz, part] + pair[1][dz, part]

        everything = slice(0, BLOCK)
        far = chip_sum(2, slope)
        ahead = chip_sum(1, slope)
        relay = [chunk(far, everything, dz).astype(bf16) for dz in range(2)]
        forth, back = move_y(relay[0], 1), move_y(relay[1], -1)
        later = after(slope, *relay)
        behind = chip_sum(3, later)
        own = chip_sum(0, after(later, behind[0]))
        both = []
        for part in (slice(0, CUT), slice(CUT, BLOCK)):
            up = [chunk(ahead, part, 0) + forth[part].astype(f32), chunk(ahead, part, 1)]
            down = [chunk(behind, part, 0), chunk(behind, part, 1) + back[part].astype(f32)]
            up = move_y(jnp.stack(up).astype(bf16), 1)
            down = move_y(jnp.stack(down).astype(bf16), -1)
            near = [
                chunk(own, part, dz) + up[dz].astype(f32) + down[dz].astype(f32)
                for dz in range(2)
            ]
            both.append((near[0], swap_z(near[1].astype(bf16))))
        top, inv0 = top_step(*both[0], prec, pc_weight)
        return low_step(*both[1], top, inv0, state, prec, prior_mean, pc_weight)

    return lax.fori_loop(0, ITERS, iterate, (state0, state0.astype(bf16)))[0]


def solution(mesh):
    return jax.shard_map(
        local,
        mesh=mesh,
        in_specs=(
            P("prof", "chan"),
            P("chan", None),
            P("prof", "chan", None),
            P("chan"),
            P("chan"),
            P("prof", "chan"),
            P(),
            P(),
            P(("prof", "chan"), None),
            P(("prof", "chan"), None),
        ),
        out_specs=P(("prof", "chan"), None),
        check_vma=False,
    )
```

time: 639 us -> 136 us (0.21)
  other arithmetic: 224 us -> 2.04 us
  blocking collectives: 208 us -> 0 us
  waiting for transfers between devices: 110 us -> 22.6 us
  starting transfers between devices: 11.3 us -> 65.4 us
  matrix products: 45 us -> 0 us
  Pallas kernels: 0 us -> 41.5 us
  between operations: 19.3 us -> 0.01 us
  local copies, waits for them, and re-layouts: 17.2 us -> 2.73 us
    another operation x40 -> x24, other arithmetic: 219 us -> 0.73 us  [the longest x8 0.25 us: iterate(): up = move_y(jnp.stack(up).astype(bf16), 1)]
    unnamed x2 -> x0, blocking collectives: 194 us -> none
    reduce_scatter x2 -> x0, waiting for transfers between devices: 103 us -> none  [local(): lax.psum_scatter(pc_jacob, 'chan', scatter_dimension=0, tiled=True)]
    ppermute x0 -> x34, starting transfers between devices: none -> 65.4 us  [the longest x6 32.8 us: swap_z(): lax.ppermute(value, 'chan', [(index_of(z, y, c), index_of(1 - z, y, c)) f...]
    pallas_call x0 -> x16, Pallas kernels: none -> 41.5 us  [the longest x2 16.9 us: low_step(): pl.pallas_call(low_kernel, out_shape=(jax.ShapeDtypeStruct(mean.shape, f3...]
    dot_general x10 -> x0, matrix products: 37.1 us -> none  [the longest x2 18.5 us: project(): jnp.einsum('rck,rcs->rks', weighted, jacobian, preferred_element_type=jnp...]
    ppermute x0 -> x34, waiting for transfers between devices: none -> 22.6 us  [the longest x18 14 us: move_y(): lax.ppermute(value, 'chan', [(index_of(z, y, c), index_of(z, (y + step) %...]
    all_to_all x1 -> x0, blocking collectives: 13.6 us -> none  [copy_for_each(): return lax.all_to_all(copies, axis, split_axis=0, concat_axis=0, tiled=True)]
  transfers between devices with their start and end apart: 3 -> 34, of which waited for: 3 -> 14; matrix products, arithmetic and copies ran while one was open for 1% -> 2% of each run, Pallas kernels for 0% -> 14%
where the time goes in v1:
time: 136 us; the launch traced here: 135 us
  starting transfers between devices  65.4 us (48%)
  Pallas kernels  41.5 us (31%)
  waiting for transfers between devices  22.6 us (17%)
  local copies, waits for them, and re-layouts  2.73 us (2%)
  other arithmetic  2.04 us (2%)
    ppermute x6, starting transfers between devices, swap_z(): lax.ppermute(value, 'chan', [(index_of(z, y, c), index_of(1 - z, y, c)) f...  32.8 us
    ppermute x18, starting transfers between devices, move_y(): lax.ppermute(value, 'chan', [(index_of(z, y, c), index_of(z, (y + step) %...  30 us
    pallas_call x2, Pallas kernels, low_step(): pl.pallas_call(low_kernel, out_shape=(jax.ShapeDtypeStruct(mean.shape, f3...  16.9 us
    ppermute x18, waiting for transfers between devices, move_y(): lax.ppermute(value, 'chan', [(index_of(z, y, c), index_of(z, (y + step) %...  14 us
    pallas_call x8, Pallas kernels, project(): pl.pallas_call(functools.partial(project_kernel, dy), out_shape=(jax.Shap...  12 us
    pallas_call x2, Pallas kernels, top_step(): pl.pallas_call(top_kernel, out_shape=(jax.ShapeDtypeStruct((TOP, 512), f3...  8.05 us
    ppermute x6, waiting for transfers between devices, swap_z(): lax.ppermute(value, 'chan', [(index_of(z, y, c), index_of(1 - z, y, c)) f...  5.34 us
    ppermute x10, waiting for transfers between devices, swap_core(): lax.ppermute(value, 'chan', [(index_of(z, y, c), index_of(z, y, 1 - c)) f...  3.29 us
  transfers between devices with their start and end apart: 34, of which 14 were waited for; matrix products, arithmetic and copies ran while one was open for 2% of the time, Pallas kernels for 14%

profile of v1, /device:TPU:2, one launch (start us, length us, event | category | flops | bytes accessed | tf_op | source)
XLA Modules:
  0.0 134.8 jit_solution(2082835347611428576)
XLA Ops:
  0.0 1.3 copy.23
  1.3 0.7 convert_element_type.75
  1.9 132.9 %while.12 = (s32[]{:T(128)}, f32[1,400]{1,0:T(1,128)}, bf16[1,400]{1,0:T(2,128)(2,1)S(1)}, s32[16,16]{1,0:T(8,128)}, bf16[16,528]{1,0:T(8,128)(2,1)}, /*index=5*...) while((s32[]{:T(128)}, f32[1,400]{1,0:T(1,128)}, ...), condition=%wide.region_1.0_spmd, body=%wide.region_0.0_spmd.sunk | while | flops 27003817984 | bytes 62125400 | solution.py:386
  1.9 1.2 collective-permute-done
  3.1 7.3 %collective-permute-start.1 = (bf16[2,400]{1,0:T(2,128)(2,1)S(1)}, bf16[2,400]{1,0:T(2,128)(2,1)S(1)}, u32[]{:S(2)}, u32[]{:S(2)}) collective-permute-start(bf16[2,400]{1,0:T(2,128)(2,1)S(1)} %pad_maximum_fusion.12), channel_id=1, source_target_pairs={{0,128},{16,144},{32,160},{48,176},{64,192},{80,208},{96,224},{112... | collective-permute-start | bytes 4808 | tf_op jit(solution)/shard_map/while/body/eval_jaxpr/ppermute | solution.py:326
  10.4 1.6 %collective-permute-done.1 = bf16[2,400]{1,0:T(2,128)(2,1)S(1)} collective-permute-done((bf16[2,400]{1,0:T(2,128)(2,1)S(1)}, bf16[2,400]{1,0:T(2,128)(2,1)S(1)}, u32[]{:S(2)}, u32[]{:S(2)}) %collective-permute-start.1) | collective-permute-done | bytes 1632 | tf_op jit(solution)/shard_map/while/body/eval_jaxpr/ppermute | solution.py:326
  12.0 1.7 %collective-permute-start.4 = (bf16[4,400]{1,0:T(4,128)(2,1)S(1)}, bf16[4,400]{1,0:T(4,128)(2,1)S(1)}, u32[]{:S(2)}, u32[]{:S(2)}) collective-permute-start(bf16[4,400]{1,0:T(4,128)(2,1)S(1)} %pad_maximum_fusion.13.refs_0_), channel_id=1, source_target_pairs={{0,32},{16,48},{32,64},{48,80},{64,96},{80,112},{96,0},{112,16},{1... | collective-permute-start | bytes 9608 | tf_op jit(solution)/shard_map/while/body/eval_jaxpr/ppermute | solution.py:320
  13.7 2.9 %collective-permute-start.3 = (bf16[4,400]{1,0:T(4,128)(2,1)S(1)}, bf16[4,400]{1,0:T(4,128)(2,1)S(1)}, u32[]{:S(2)}, u32[]{:S(2)}) collective-permute-start(bf16[4,400]{1,0:T(4,128)(2,1)S(1)} %pad_maximum_fusion.13.refs_0_), channel_id=1, source_target_pairs={{0,64},{16,80},{32,96},{48,112},{64,0},{80,16},{96,32},{112,48},{1... | collective-permute-start | bytes 9608 | tf_op jit(solution)/shard_map/while/body/eval_jaxpr/ppermute | solution.py:320
  16.6 1.3 %collective-permute-start.2 = (bf16[4,400]{1,0:T(4,128)(2,1)S(1)}, bf16[4,400]{1,0:T(4,128)(2,1)S(1)}, u32[]{:S(2)}, u32[]{:S(2)}) collective-permute-start(bf16[4,400]{1,0:T(4,128)(2,1)S(1)} %pad_maximum_fusion.13.refs_0_), channel_id=1, source_target_pairs={{0,96},{16,112},{32,0},{48,16},{64,32},{80,48},{96,64},{112,80},{1... | collective-permute-start | bytes 9608 | tf_op jit(solution)/shard_map/while/body/eval_jaxpr/ppermute | solution.py:320
  17.9 0.8 valid_channels.1.refs_5_
  18.8 1.4 %collective-permute-done.2.refs_1_ = bf16[4,400]{1,0:T(4,128)(2,1)S(1)} collective-permute-done((bf16[4,400]{1,0:T(4,128)(2,1)S(1)}, bf16[4,400]{1,0:T(4,128)(2,1)S(1)}, u32[]{:S(2)}, u32[]{:S(2)}) %collective-permute-start.2) | collective-permute-done | bytes 3232 | tf_op jit(solution)/shard_map/while/body/eval_jaxpr/ppermute | solution.py:320
  20.3 1.4 %slopes.1 = (f32[16,528]{1,0:T(8,128)S(1)}, f32[16,384]{1,0:T(8,128)S(1)}) custom-call(bf16[4,400]{1,0:T(4,128)(2,1)S(1)} %pad_maximum_fusion.13.refs_0_, bf16[4,400]{1,0:T(4,128)(2,1)S(1)} %collective-permute-done.2.refs_1_, bf16[4,400]{1,0:T(4,128)(2,1)S(1)} %collective-permute-done.3.refs_2_, bf16[4,400]{1,0:T(4,128)(2,1)S(1)} %collective-permute-done.4.refs_3_, ...), custom_call_target="tpu_custom_call" | custom-call | flops 1000000000 | tf_op jit(solution)/shard_map/while/body/eval_jaxpr/slopes/pallas_call | solution.py:81
  21.7 1.5 %project.4 = (f32[2,960,128]{2,1,0:T(8,128)S(1)}, f32[2,960,128]{2,1,0:T(8,128)S(1)}) custom-call(f32[16,528]{1,0:T(8,128)S(1)} %get-tuple-element.220.slope_ref, f32[16,384]{1,0:T(8,128)S(1)} %get-tuple-element.213.resid_ref, bf16[300,528]{1,0:T(8,128)(2,1)S(1)} %copy-done, bf16[16,400,528]{2,1,0:T(8,128)(2,1)S(1)} %bitcast.79), custom_call_target="tpu_custom_call" | custom-call | flops 1000000000 | tf_op jit(solution)/shard_map/while/body/eval_jaxpr/project/pallas_call | solution.py:135
  23.3 1.5 %project.7 = (f32[2,960,128]{2,1,0:T(8,128)S(1)}, f32[2,960,128]{2,1,0:T(8,128)S(1)}) custom-call(f32[16,528]{1,0:T(8,128)S(1)} %get-tuple-element.220.slope_ref, f32[16,384]{1,0:T(8,128)S(1)} %get-tuple-element.213.resid_ref, bf16[300,528]{1,0:T(8,128)(2,1)S(1)} %copy-done, bf16[16,400,528]{2,1,0:T(8,128)(2,1)S(1)} %bitcast.79), custom_call_target="tpu_custom_call" | custom-call | flops 1000000000 | tf_op jit(solution)/shard_map/while/body/eval_jaxpr/project/pallas_call | solution.py:135
  26.3 3.1 %collective-permute-start.8 = (bf16[960,128]{1,0:T(8,128)(2,1)S(1)}, bf16[960,128]{1,0:T(8,128)(2,1)S(1)}, u32[]{:S(2)}, u32[]{:S(2)}) collective-permute-start(bf16[960,128]{1,0:T(8,128)(2,1)S(1)} %get-tuple-element.217), channel_id=1, source_target_pairs={{0,96},{16,112},{32,0},{48,16},{64,32},{80,48},{96,64},{112,80},{1... | collective-permute-start | bytes 737288 | tf_op jit(solution)/shard_map/while/body/eval_jaxpr/ppermute | solution.py:320
  29.3 1.5 %project.5 = (f32[2,960,128]{2,1,0:T(8,128)S(1)}, f32[2,960,128]{2,1,0:T(8,128)S(1)}) custom-call(f32[16,528]{1,0:T(8,128)S(1)} %get-tuple-element.220.slope_ref, f32[16,384]{1,0:T(8,128)S(1)} %get-tuple-element.213.resid_ref, bf16[300,528]{1,0:T(8,128)(2,1)S(1)} %copy-done, bf16[16,400,528]{2,1,0:T(8,128)(2,1)S(1)} %bitcast.79), custom_call_target="tpu_custom_call" | custom-call | flops 1000000000 | tf_op jit(solution)/shard_map/while/body/eval_jaxpr/project/pallas_call | solution.py:135
  30.9 1.5 %project.6 = (f32[2,960,128]{2,1,0:T(8,128)S(1)}, f32[2,960,128]{2,1,0:T(8,128)S(1)}) custom-call(f32[16,528]{1,0:T(8,128)S(1)} %get-tuple-element.220.slope_ref, f32[16,384]{1,0:T(8,128)S(1)} %get-tuple-element.213.resid_ref, bf16[300,528]{1,0:T(8,128)(2,1)S(1)} %copy-done, bf16[16,400,528]{2,1,0:T(8,128)(2,1)S(1)} %bitcast.79), custom_call_target="tpu_custom_call" | custom-call | flops 1000000000 | tf_op jit(solution)/shard_map/while/body/eval_jaxpr/project/pallas_call | solution.py:135
  33.1 2.2 %collective-permute-done.11 = bf16[960,128]{1,0:T(8,128)(2,1)S(1)} collective-permute-done((bf16[960,128]{1,0:T(8,128)(2,1)S(1)}, bf16[960,128]{1,0:T(8,128)(2,1)S(1)}, u32[]{:S(2)}, u32[]{:S(2)}) %collective-permute-start.11) | collective-permute-done | bytes 245792 | tf_op jit(solution)/shard_map/while/body/eval_jaxpr/ppermute | solution.py:320
  36.0 3.1 %collective-permute-start.14 = (bf16[2,400,128]{2,1,0:T(8,128)(2,1)S(1)}, bf16[2,400,128]{2,1,0:T(8,128)(2,1)S(1)}, u32[]{:S(2)}, u32[]{:S(2)}) collective-permute-start(bf16[2,400,128]{2,1,0:T(8,128)(2,1)S(1)} %pad_maximum_fusion.16), channel_id=1, source_target_pairs={{0,96},{16,112},{32,0},{48,16},{64,32},{80,48},{96,64},{112,80},{1... | collective-permute-start | bytes 614408 | tf_op jit(solution)/shard_map/while/body/eval_jaxpr/ppermute | solution.py:320
  39.1 2.1 %collective-permute-start.9 = (bf16[2,560,128]{2,1,0:T(8,128)(2,1)S(1)}, bf16[2,560,128]{2,1,0:T(8,128)(2,1)S(1)}, u32[]{:S(2)}, u32[]{:S(2)}) collective-permute-start(bf16[2,560,128]{2,1,0:T(8,128)(2,1)S(1)} %pad_maximum_fusion.14), channel_id=1, source_target_pairs={{0,96},{16,112},{32,0},{48,16},{64,32},{80,48},{96,64},{112,80},{1... | collective-permute-start | bytes 860168 | tf_op jit(solution)/shard_map/while/body/eval_jaxpr/ppermute | solution.py:320
  41.2 3.4 %collective-permute-done.15 = bf16[2,400,128]{2,1,0:T(8,128)(2,1)S(1)} collective-permute-done((bf16[2,400,128]{2,1,0:T(8,128)(2,1)S(1)}, bf16[2,400,128]{2,1,0:T(8,128)(2,1)S(1)}, u32[]{:S(2)}, u32[]{:S(2)}) %collective-permute-start.15) | collective-permute-done | bytes 204832 | tf_op jit(solution)/shard_map/while/body/eval_jaxpr/ppermute | solution.py:320
  44.7 6.0 %collective-permute-start.16 = (bf16[400,128]{1,0:T(8,128)(2,1)S(1)}, bf16[400,128]{1,0:T(8,128)(2,1)S(1)}, u32[]{:S(2)}, u32[]{:S(2)}) collective-permute-start(bf16[400,128]{1,0:T(8,128)(2,1)S(1)} %get-tuple-element.229), channel_id=1, source_target_pairs={{0,128},{16,144},{32,160},{48,176},{64,192},{80,208},{96,224},{112... | collective-permute-start | bytes 307208 | tf_op jit(solution)/shard_map/while/body/eval_jaxpr/ppermute | solution.py:326
  50.8 4.4 %collective-permute-start.13 = (bf16[560,128]{1,0:T(8,128)(2,1)S(1)}, bf16[560,128]{1,0:T(8,128)(2,1)S(1)}, u32[]{:S(2)}, u32[]{:S(2)}) collective-permute-start(bf16[560,128]{1,0:T(8,128)(2,1)S(1)} %get-tuple-element.227), channel_id=1, source_target_pairs={{0,128},{16,144},{32,160},{48,176},{64,192},{80,208},{96,224},{112... | collective-permute-start | bytes 430088 | tf_op jit(solution)/shard_map/while/body/eval_jaxpr/ppermute | solution.py:326
  55.9 4.0 %top_step.1 = (f32[128,512]{1,0:T(8,128)S(1)}, f32[128,128]{1,0:T(8,128)S(1)}) custom-call(f32[400,128]{1,0:T(8,128)S(1)} %get-tuple-element.228.keep_ref, bf16[400,128]{1,0:T(8,128)(2,1)S(1)} %collective-permute-done.16.got_ref, f32[1,400]{1,0:T(1,128)S(1)} %copy-done.4, f32[300]{0:T(512)S(1)} %copy-done.5), custom_call_target="tpu_custom_call" | custom-call | flops 1000000000 | tf_op jit(solution)/shard_map/while/body/eval_jaxpr/top_step/pallas_call | solution.py:241
  60.2 8.5 %low_step.1 = (f32[1,400]{1,0:T(1,128)}, bf16[1,400]{1,0:T(2,128)(2,1)S(1)}) custom-call(f32[560,128]{1,0:T(8,128)S(1)} %get-tuple-element.226.keep_ref, bf16[560,128]{1,0:T(8,128)(2,1)S(1)} %collective-permute-done.13.got_ref, f32[128,512]{1,0:T(8,128)S(1)} %get-tuple-element.230.top_ref, f32[128,128]{1,0:T(8,128)S(1)} %get-tuple-element.231.inv_ref, ...), custom_call_target="tpu_custom_call" | custom-call | flops 1000000000 | tf_op jit(solution)/shard_map/while/body/eval_jaxpr/low_step/pallas_call | solution.py:294
  68.7 1.2 collective-permute-done
  69.9 5.6 %collective-permute-start.1 = (bf16[2,400]{1,0:T(2,128)(2,1)S(1)}, bf16[2,400]{1,0:T(2,128)(2,1)S(1)}, u32[]{:S(2)}, u32[]{:S(2)}) collective-permute-start(bf16[2,400]{1,0:T(2,128)(2,1)S(1)} %pad_maximum_fusion.12), channel_id=1, source_target_pairs={{0,128},{16,144},{32,160},{48,176},{64,192},{80,208},{96,224},{112... | collective-permute-start | bytes 4808 | tf_op jit(solution)/shard_map/while/body/eval_jaxpr/ppermute | solution.py:326
  75.4 2.0 %collective-permute-done.1 = bf16[2,400]{1,0:T(2,128)(2,1)S(1)} collective-permute-done((bf16[2,400]{1,0:T(2,128)(2,1)S(1)}, bf16[2,400]{1,0:T(2,128)(2,1)S(1)}, u32[]{:S(2)}, u32[]{:S(2)}) %collective-permute-start.1) | collective-permute-done | bytes 1632 | tf_op jit(solution)/shard_map/while/body/eval_jaxpr/ppermute | solution.py:326
  77.5 1.8 %collective-permute-start.4 = (bf16[4,400]{1,0:T(4,128)(2,1)S(1)}, bf16[4,400]{1,0:T(4,128)(2,1)S(1)}, u32[]{:S(2)}, u32[]{:S(2)}) collective-permute-start(bf16[4,400]{1,0:T(4,128)(2,1)S(1)} %pad_maximum_fusion.13.refs_0_), channel_id=1, source_target_pairs={{0,32},{16,48},{32,64},{48,80},{64,96},{80,112},{96,0},{112,16},{1... | collective-permute-start | bytes 9608 | tf_op jit(solution)/shard_map/while/body/eval_jaxpr/ppermute | solution.py:320
  79.3 3.2 %collective-permute-start.3 = (bf16[4,400]{1,0:T(4,128)(2,1)S(1)}, bf16[4,400]{1,0:T(4,128)(2,1)S(1)}, u32[]{:S(2)}, u32[]{:S(2)}) collective-permute-start(bf16[4,400]{1,0:T(4,128)(2,1)S(1)} %pad_maximum_fusion.13.refs_0_), channel_id=1, source_target_pairs={{0,64},{16,80},{32,96},{48,112},{64,0},{80,16},{96,32},{112,48},{1... | collective-permute-start | bytes 9608 | tf_op jit(solution)/shard_map/while/body/eval_jaxpr/ppermute | solution.py:320
  82.4 1.4 %collective-permute-start.2 = (bf16[4,400]{1,0:T(4,128)(2,1)S(1)}, bf16[4,400]{1,0:T(4,128)(2,1)S(1)}, u32[]{:S(2)}, u32[]{:S(2)}) collective-permute-start(bf16[4,400]{1,0:T(4,128)(2,1)S(1)} %pad_maximum_fusion.13.refs_0_), channel_id=1, source_target_pairs={{0,96},{16,112},{32,0},{48,16},{64,32},{80,48},{96,64},{112,80},{1... | collective-permute-start | bytes 9608 | tf_op jit(solution)/shard_map/while/body/eval_jaxpr/ppermute | solution.py:320
  83.8 0.8 valid_channels.1.refs_5_
  84.7 1.4 %collective-permute-done.2.refs_1_ = bf16[4,400]{1,0:T(4,128)(2,1)S(1)} collective-permute-done((bf16[4,400]{1,0:T(4,128)(2,1)S(1)}, bf16[4,400]{1,0:T(4,128)(2,1)S(1)}, u32[]{:S(2)}, u32[]{:S(2)}) %collective-permute-start.2) | collective-permute-done | bytes 3232 | tf_op jit(solution)/shard_map/while/body/eval_jaxpr/ppermute | solution.py:320
  86.1 1.4 %slopes.1 = (f32[16,528]{1,0:T(8,128)S(1)}, f32[16,384]{1,0:T(8,128)S(1)}) custom-call(bf16[4,400]{1,0:T(4,128)(2,1)S(1)} %pad_maximum_fusion.13.refs_0_, bf16[4,400]{1,0:T(4,128)(2,1)S(1)} %collective-permute-done.2.refs_1_, bf16[4,400]{1,0:T(4,128)(2,1)S(1)} %collective-permute-done.3.refs_2_, bf16[4,400]{1,0:T(4,128)(2,1)S(1)} %collective-permute-done.4.refs_3_, ...), custom_call_target="tpu_custom_call" | custom-call | flops 1000000000 | tf_op jit(solution)/shard_map/while/body/eval_jaxpr/slopes/pallas_call | solution.py:81
  87.6 1.5 %project.4 = (f32[2,960,128]{2,1,0:T(8,128)S(1)}, f32[2,960,128]{2,1,0:T(8,128)S(1)}) custom-call(f32[16,528]{1,0:T(8,128)S(1)} %get-tuple-element.220.slope_ref, f32[16,384]{1,0:T(8,128)S(1)} %get-tuple-element.213.resid_ref, bf16[300,528]{1,0:T(8,128)(2,1)S(1)} %copy-done, bf16[16,400,528]{2,1,0:T(8,128)(2,1)S(1)} %bitcast.79), custom_call_target="tpu_custom_call" | custom-call | flops 1000000000 | tf_op jit(solution)/shard_map/while/body/eval_jaxpr/project/pallas_call | solution.py:135
  89.2 1.5 %project.7 = (f32[2,960,128]{2,1,0:T(8,128)S(1)}, f32[2,960,128]{2,1,0:T(8,128)S(1)}) custom-call(f32[16,528]{1,0:T(8,128)S(1)} %get-tuple-element.220.slope_ref, f32[16,384]{1,0:T(8,128)S(1)} %get-tuple-element.213.resid_ref, bf16[300,528]{1,0:T(8,128)(2,1)S(1)} %copy-done, bf16[16,400,528]{2,1,0:T(8,128)(2,1)S(1)} %bitcast.79), custom_call_target="tpu_custom_call" | custom-call | flops 1000000000 | tf_op jit(solution)/shard_map/while/body/eval_jaxpr/project/pallas_call | solution.py:135
  92.1 3.0 %collective-permute-start.8 = (bf16[960,128]{1,0:T(8,128)(2,1)S(1)}, bf16[960,128]{1,0:T(8,128)(2,1)S(1)}, u32[]{:S(2)}, u32[]{:S(2)}) collective-permute-start(bf16[960,128]{1,0:T(8,128)(2,1)S(1)} %get-tuple-element.217), channel_id=1, source_target_pairs={{0,96},{16,112},{32,0},{48,16},{64,32},{80,48},{96,64},{112,80},{1... | collective-permute-start | bytes 737288 | tf_op jit(solution)/shard_map/while/body/eval_jaxpr/ppermute | solution.py:320
  95.1 1.5 %project.5 = (f32[2,960,128]{2,1,0:T(8,128)S(1)}, f32[2,960,128]{2,1,0:T(8,128)S(1)}) custom-call(f32[16,528]{1,0:T(8,128)S(1)} %get-tuple-element.220.slope_ref, f32[16,384]{1,0:T(8,128)S(1)} %get-tuple-element.213.resid_ref, bf16[300,528]{1,0:T(8,128)(2,1)S(1)} %copy-done, bf16[16,400,528]{2,1,0:T(8,128)(2,1)S(1)} %bitcast.79), custom_call_target="tpu_custom_call" | custom-call | flops 1000000000 | tf_op jit(solution)/shard_map/while/body/eval_jaxpr/project/pallas_call | solution.py:135
  96.8 1.5 %project.6 = (f32[2,960,128]{2,1,0:T(8,128)S(1)}, f32[2,960,128]{2,1,0:T(8,128)S(1)}) custom-call(f32[16,528]{1,0:T(8,128)S(1)} %get-tuple-element.220.slope_ref, f32[16,384]{1,0:T(8,128)S(1)} %get-tuple-element.213.resid_ref, bf16[300,528]{1,0:T(8,128)(2,1)S(1)} %copy-done, bf16[16,400,528]{2,1,0:T(8,128)(2,1)S(1)} %bitcast.79), custom_call_target="tpu_custom_call" | custom-call | flops 1000000000 | tf_op jit(solution)/shard_map/while/body/eval_jaxpr/project/pallas_call | solution.py:135
  98.9 2.2 %collective-permute-done.11 = bf16[960,128]{1,0:T(8,128)(2,1)S(1)} collective-permute-done((bf16[960,128]{1,0:T(8,128)(2,1)S(1)}, bf16[960,128]{1,0:T(8,128)(2,1)S(1)}, u32[]{:S(2)}, u32[]{:S(2)}) %collective-permute-start.11) | collective-permute-done | bytes 245792 | tf_op jit(solution)/shard_map/while/body/eval_jaxpr/ppermute | solution.py:320
  101.9 3.0 %collective-permute-start.14 = (bf16[2,400,128]{2,1,0:T(8,128)(2,1)S(1)}, bf16[2,400,128]{2,1,0:T(8,128)(2,1)S(1)}, u32[]{:S(2)}, u32[]{:S(2)}) collective-permute-start(bf16[2,400,128]{2,1,0:T(8,128)(2,1)S(1)} %pad_maximum_fusion.16), channel_id=1, source_target_pairs={{0,96},{16,112},{32,0},{48,16},{64,32},{80,48},{96,64},{112,80},{1... | collective-permute-start | bytes 614408 | tf_op jit(solution)/shard_map/while/body/eval_jaxpr/ppermute | solution.py:320
  105.0 2.1 %collective-permute-start.9 = (bf16[2,560,128]{2,1,0:T(8,128)(2,1)S(1)}, bf16[2,560,128]{2,1,0:T(8,128)(2,1)S(1)}, u32[]{:S(2)}, u32[]{:S(2)}) collective-permute-start(bf16[2,560,128]{2,1,0:T(8,128)(2,1)S(1)} %pad_maximum_fusion.14), channel_id=1, source_target_pairs={{0,96},{16,112},{32,0},{48,16},{64,32},{80,48},{96,64},{112,80},{1... | collective-permute-start | bytes 860168 | tf_op jit(solution)/shard_map/while/body/eval_jaxpr/ppermute | solution.py:320
  107.1 3.4 %collective-permute-done.15 = bf16[2,400,128]{2,1,0:T(8,128)(2,1)S(1)} collective-permute-done((bf16[2,400,128]{2,1,0:T(8,128)(2,1)S(1)}, bf16[2,400,128]{2,1,0:T(8,128)(2,1)S(1)}, u32[]{:S(2)}, u32[]{:S(2)}) %collective-permute-start.15) | collective-permute-done | bytes 204832 | tf_op jit(solution)/shard_map/while/body/eval_jaxpr/ppermute | solution.py:320
  110.5 5.3 %collective-permute-start.16 = (bf16[400,128]{1,0:T(8,128)(2,1)S(1)}, bf16[400,128]{1,0:T(8,128)(2,1)S(1)}, u32[]{:S(2)}, u32[]{:S(2)}) collective-permute-start(bf16[400,128]{1,0:T(8,128)(2,1)S(1)} %get-tuple-element.229), channel_id=1, source_target_pairs={{0,128},{16,144},{32,160},{48,176},{64,192},{80,208},{96,224},{112... | collective-permute-start | bytes 307208 | tf_op jit(solution)/shard_map/while/body/eval_jaxpr/ppermute | solution.py:326
  116.0 4.2 %collective-permute-start.13 = (bf16[560,128]{1,0:T(8,128)(2,1)S(1)}, bf16[560,128]{1,0:T(8,128)(2,1)S(1)}, u32[]{:S(2)}, u32[]{:S(2)}) collective-permute-start(bf16[560,128]{1,0:T(8,128)(2,1)S(1)} %get-tuple-element.227), channel_id=1, source_target_pairs={{0,128},{16,144},{32,160},{48,176},{64,192},{80,208},{96,224},{112... | collective-permute-start | bytes 430088 | tf_op jit(solution)/shard_map/while/body/eval_jaxpr/ppermute | solution.py:326
  120.9 4.0 %top_step.1 = (f32[128,512]{1,0:T(8,128)S(1)}, f32[128,128]{1,0:T(8,128)S(1)}) custom-call(f32[400,128]{1,0:T(8,128)S(1)} %get-tuple-element.228.keep_ref, bf16[400,128]{1,0:T(8,128)(2,1)S(1)} %collective-permute-done.16.got_ref, f32[1,400]{1,0:T(1,128)S(1)} %copy-done.4, f32[300]{0:T(512)S(1)} %copy-done.5), custom_call_target="tpu_custom_call" | custom-call | flops 1000000000 | tf_op jit(solution)/shard_map/while/body/eval_jaxpr/top_step/pallas_call | solution.py:241
  124.9 1.4 %collective-permute-done.13.got_ref = bf16[560,128]{1,0:T(8,128)(2,1)S(1)} collective-permute-done((bf16[560,128]{1,0:T(8,128)(2,1)S(1)}, bf16[560,128]{1,0:T(8,128)(2,1)S(1)}, u32[]{:S(2)}, u32[]{:S(2)}) %collective-permute-start.13) | collective-permute-done | bytes 143392 | tf_op jit(solution)/shard_map/while/body/eval_jaxpr/ppermute | solution.py:326
  126.4 8.5 %low_step.1 = (f32[1,400]{1,0:T(1,128)}, bf16[1,400]{1,0:T(2,128)(2,1)S(1)}) custom-call(f32[560,128]{1,0:T(8,128)S(1)} %get-tuple-element.226.keep_ref, bf16[560,128]{1,0:T(8,128)(2,1)S(1)} %collective-permute-done.13.got_ref, f32[128,512]{1,0:T(8,128)S(1)} %get-tuple-element.230.top_ref, f32[128,128]{1,0:T(8,128)S(1)} %get-tuple-element.231.inv_ref, ...), custom_call_target="tpu_custom_call" | custom-call | flops 1000000000 | tf_op jit(solution)/shard_map/while/body/eval_jaxpr/low_step/pallas_call | solution.py:294
  (113 shorter events, 8.3 us)
Async XLA Ops:
  1.9 1.2 collective-permute-start
  3.1 8.8 %collective-permute-start.1 = (bf16[2,400]{1,0:T(2,128)(2,1)S(1)}, bf16[2,400]{1,0:T(2,128)(2,1)S(1)}, u32[]{:S(2)}, u32[]{:S(2)}) collective-permute-start(bf16[2,400]{1,0:T(2,128)(2,1)S(1)} %pad_maximum_fusion.12), channel_id=1, source_target_pairs={{0,128},{16,144},{32,160},{48,176},{64,192},{80,208},{96,224},{112... | collective-permute-start | bytes 4808 | tf_op jit(solution)/shard_map/while/body/eval_jaxpr/ppermute | solution.py:326
  12.0 8.2 %slice-start = ((s8[8192000]{0:T(1024)(128)(4,1)}), s8[4194304]{0:T(1024)(128)(4,1)S(1)}, s32[]{:S(2)}) async-start(s8[8192000]{0:T(1024)(128)(4,1)} %bitcast.78), calls=%async_computation | async-start | bytes 8388608 | tf_op jit(solution)/shard_map/while
  12.0 8.2 %slice-start.1 = ((s8[8192000]{0:T(1024)(128)(4,1)}), s8[3997696]{0:T(1024)(128)(4,1)S(1)}, s32[]{:S(2)}) async-start(s8[8192000]{0:T(1024)(128)(4,1)} %bitcast.78), calls=%async_computation.1 | async-start | bytes 7995392 | tf_op jit(solution)/shard_map/while
  12.0 6.7 %collective-permute-start.4 = (bf16[4,400]{1,0:T(4,128)(2,1)S(1)}, bf16[4,400]{1,0:T(4,128)(2,1)S(1)}, u32[]{:S(2)}, u32[]{:S(2)}) collective-permute-start(bf16[4,400]{1,0:T(4,128)(2,1)S(1)} %pad_maximum_fusion.13.refs_0_), channel_id=1, source_target_pairs={{0,32},{16,48},{32,64},{48,80},{64,96},{80,112},{96,0},{112,16},{1... | collective-permute-start | bytes 9608 | tf_op jit(solution)/shard_map/while/body/eval_jaxpr/ppermute | solution.py:320
  13.7 5.1 %collective-permute-start.3 = (bf16[4,400]{1,0:T(4,128)(2,1)S(1)}, bf16[4,400]{1,0:T(4,128)(2,1)S(1)}, u32[]{:S(2)}, u32[]{:S(2)}) collective-permute-start(bf16[4,400]{1,0:T(4,128)(2,1)S(1)} %pad_maximum_fusion.13.refs_0_), channel_id=1, source_target_pairs={{0,64},{16,80},{32,96},{48,112},{64,0},{80,16},{96,32},{112,48},{1... | collective-permute-start | bytes 9608 | tf_op jit(solution)/shard_map/while/body/eval_jaxpr/ppermute | solution.py:320
  16.6 3.6 %collective-permute-start.2 = (bf16[4,400]{1,0:T(4,128)(2,1)S(1)}, bf16[4,400]{1,0:T(4,128)(2,1)S(1)}, u32[]{:S(2)}, u32[]{:S(2)}) collective-permute-start(bf16[4,400]{1,0:T(4,128)(2,1)S(1)} %pad_maximum_fusion.13.refs_0_), channel_id=1, source_target_pairs={{0,96},{16,112},{32,0},{48,16},{64,32},{80,48},{96,64},{112,80},{1... | collective-permute-start | bytes 9608 | tf_op jit(solution)/shard_map/while/body/eval_jaxpr/ppermute | solution.py:320
  23.2 2.7 %collective-permute-start.5 = (f32[2,960,128]{2,1,0:T(8,128)S(1)}, f32[2,960,128]{2,1,0:T(8,128)S(1)}, u32[]{:S(2)}, u32[]{:S(2)}) collective-permute-start(f32[2,960,128]{2,1,0:T(8,128)S(1)} %get-tuple-element.214), channel_id=1, source_target_pairs={{0,16},{16,0},{32,48},{48,32},{64,80},{80,64},{96,112},{112,96},{1... | collective-permute-start | bytes 2949128 | tf_op jit(solution)/shard_map/while/body/eval_jaxpr/ppermute | solution.py:314
  24.8 8.2 %collective-permute-start.10 = (f32[2,960,128]{2,1,0:T(8,128)S(1)}, f32[2,960,128]{2,1,0:T(8,128)S(1)}, u32[]{:S(2)}, u32[]{:S(2)}) collective-permute-start(f32[2,960,128]{2,1,0:T(8,128)S(1)} %get-tuple-element.224), channel_id=1, source_target_pairs={{0,16},{16,0},{32,48},{48,32},{64,80},{80,64},{96,112},{112,96},{1... | collective-permute-start | bytes 2949128 | tf_op jit(solution)/shard_map/while/body/eval_jaxpr/ppermute | solution.py:314
  26.0 9.3 %collective-permute-start.11 = (bf16[960,128]{1,0:T(8,128)(2,1)S(1)}, bf16[960,128]{1,0:T(8,128)(2,1)S(1)}, u32[]{:S(2)}, u32[]{:S(2)}) collective-permute-start(bf16[960,128]{1,0:T(8,128)(2,1)S(1)} %get-tuple-element.216), channel_id=1, source_target_pairs={{0,32},{16,48},{32,64},{48,80},{64,96},{80,112},{96,0},{112,16},{1... | collective-permute-start | bytes 737288 | tf_op jit(solution)/shard_map/while/body/eval_jaxpr/ppermute | solution.py:320
  26.3 9.6 %collective-permute-start.8 = (bf16[960,128]{1,0:T(8,128)(2,1)S(1)}, bf16[960,128]{1,0:T(8,128)(2,1)S(1)}, u32[]{:S(2)}, u32[]{:S(2)}) collective-permute-start(bf16[960,128]{1,0:T(8,128)(2,1)S(1)} %get-tuple-element.217), channel_id=1, source_target_pairs={{0,96},{16,112},{32,0},{48,16},{64,32},{80,48},{96,64},{112,80},{1... | collective-permute-start | bytes 737288 | tf_op jit(solution)/shard_map/while/body/eval_jaxpr/ppermute | solution.py:320
  30.8 25.1 %copy-start.4 = (f32[1,400]{1,0:T(1,128)S(1)}, f32[1,400]{1,0:T(1,128)}, u32[]{:S(2)}) copy-start(f32[1,400]{1,0:T(1,128)} %get-tuple-element.269.prec_ref) | copy-start | bytes 4804 | tf_op jit(solution)/shard_map/while
  30.8 25.1 %copy-start.5 = (f32[300]{0:T(512)S(1)}, f32[300]{0:T(512)}, u32[]{:S(2)}) copy-start(f32[300]{0:T(512)} %get-tuple-element.270.weight_ref) | copy-start | bytes 3604 | tf_op jit(solution)/shard_map/while
  30.8 5.1 %collective-permute-start.7 = (f32[2,960,128]{2,1,0:T(8,128)S(1)}, f32[2,960,128]{2,1,0:T(8,128)S(1)}, u32[]{:S(2)}, u32[]{:S(2)}) collective-permute-start(f32[2,960,128]{2,1,0:T(8,128)S(1)} %get-tuple-element.223), channel_id=1, source_target_pairs={{0,16},{16,0},{32,48},{48,32},{64,80},{80,64},{96,112},{112,96},{1... | collective-permute-start | bytes 2949128 | tf_op jit(solution)/shard_map/while/body/eval_jaxpr/ppermute | solution.py:314
  32.4 27.8 %copy-start.6 = (f32[1,400]{1,0:T(1,128)S(1)}, f32[1,400]{1,0:T(1,128)}, u32[]{:S(2)}) copy-start(f32[1,400]{1,0:T(1,128)} %get-tuple-element.271.mean_ref) | copy-start | bytes 4804 | tf_op jit(solution)/shard_map/while
  32.4 12.1 %collective-permute-start.6 = (f32[2,960,128]{2,1,0:T(8,128)S(1)}, f32[2,960,128]{2,1,0:T(8,128)S(1)}, u32[]{:S(2)}, u32[]{:S(2)}) collective-permute-start(f32[2,960,128]{2,1,0:T(8,128)S(1)} %get-tuple-element.221), channel_id=1, source_target_pairs={{0,16},{16,0},{32,48},{48,32},{64,80},{80,64},{96,112},{112,96},{1... | collective-permute-start | bytes 2949128 | tf_op jit(solution)/shard_map/while/body/eval_jaxpr/ppermute | solution.py:314
  35.3 9.2 %collective-permute-start.15 = (bf16[2,400,128]{2,1,0:T(8,128)(2,1)S(1)}, bf16[2,400,128]{2,1,0:T(8,128)(2,1)S(1)}, u32[]{:S(2)}, u32[]{:S(2)}) collective-permute-start(bf16[2,400,128]{2,1,0:T(8,128)(2,1)S(1)} %pad_maximum_fusion.17), channel_id=1, source_target_pairs={{0,32},{16,48},{32,64},{48,80},{64,96},{80,112},{96,0},{112,16},{1... | collective-permute-start | bytes 614408 | tf_op jit(solution)/shard_map/while/body/eval_jaxpr/ppermute | solution.py:320
  35.5 15.2 %collective-permute-start.12 = (bf16[2,560,128]{2,1,0:T(8,128)(2,1)S(1)}, bf16[2,560,128]{2,1,0:T(8,128)(2,1)S(1)}, u32[]{:S(2)}, u32[]{:S(2)}) collective-permute-start(bf16[2,560,128]{2,1,0:T(8,128)(2,1)S(1)} %pad_maximum_fusion.15), channel_id=1, source_target_pairs={{0,32},{16,48},{32,64},{48,80},{64,96},{80,112},{96,0},{112,16},{1... | collective-permute-start | bytes 860168 | tf_op jit(solution)/shard_map/while/body/eval_jaxpr/ppermute | solution.py:320
  36.0 8.6 %collective-permute-start.14 = (bf16[2,400,128]{2,1,0:T(8,128)(2,1)S(1)}, bf16[2,400,128]{2,1,0:T(8,128)(2,1)S(1)}, u32[]{:S(2)}, u32[]{:S(2)}) collective-permute-start(bf16[2,400,128]{2,1,0:T(8,128)(2,1)S(1)} %pad_maximum_fusion.16), channel_id=1, source_target_pairs={{0,96},{16,112},{32,0},{48,16},{64,32},{80,48},{96,64},{112,80},{1... | collective-permute-start | bytes 614408 | tf_op jit(solution)/shard_map/while/body/eval_jaxpr/ppermute | solution.py:320
  39.1 11.5 %collective-permute-start.9 = (bf16[2,560,128]{2,1,0:T(8,128)(2,1)S(1)}, bf16[2,560,128]{2,1,0:T(8,128)(2,1)S(1)}, u32[]{:S(2)}, u32[]{:S(2)}) collective-permute-start(bf16[2,560,128]{2,1,0:T(8,128)(2,1)S(1)} %pad_maximum_fusion.14), channel_id=1, source_target_pairs={{0,96},{16,112},{32,0},{48,16},{64,32},{80,48},{96,64},{112,80},{1... | collective-permute-start | bytes 860168 | tf_op jit(solution)/shard_map/while/body/eval_jaxpr/ppermute | solution.py:320
  44.7 11.2 %collective-permute-start.16 = (bf16[400,128]{1,0:T(8,128)(2,1)S(1)}, bf16[400,128]{1,0:T(8,128)(2,1)S(1)}, u32[]{:S(2)}, u32[]{:S(2)}) collective-permute-start(bf16[400,128]{1,0:T(8,128)(2,1)S(1)} %get-tuple-element.229), channel_id=1, source_target_pairs={{0,128},{16,144},{32,160},{48,176},{64,192},{80,208},{96,224},{112... | collective-permute-start | bytes 307208 | tf_op jit(solution)/shard_map/while/body/eval_jaxpr/ppermute | solution.py:326
  50.8 9.4 %collective-permute-start.13 = (bf16[560,128]{1,0:T(8,128)(2,1)S(1)}, bf16[560,128]{1,0:T(8,128)(2,1)S(1)}, u32[]{:S(2)}, u32[]{:S(2)}) collective-permute-start(bf16[560,128]{1,0:T(8,128)(2,1)S(1)} %get-tuple-element.227), channel_id=1, source_target_pairs={{0,128},{16,144},{32,160},{48,176},{64,192},{80,208},{96,224},{112... | collective-permute-start | bytes 430088 | tf_op jit(solution)/shard_map/while/body/eval_jaxpr/ppermute | solution.py:326
  68.7 1.2 collective-permute-start
  69.9 7.6 %collective-permute-start.1 = (bf16[2,400]{1,0:T(2,128)(2,1)S(1)}, bf16[2,400]{1,0:T(2,128)(2,1)S(1)}, u32[]{:S(2)}, u32[]{:S(2)}) collective-permute-start(bf16[2,400]{1,0:T(2,128)(2,1)S(1)} %pad_maximum_fusion.12), channel_id=1, source_target_pairs={{0,128},{16,144},{32,160},{48,176},{64,192},{80,208},{96,224},{112... | collective-permute-start | bytes 4808 | tf_op jit(solution)/shard_map/while/body/eval_jaxpr/ppermute | solution.py:326
  77.4 8.6 %slice-start = ((s8[8192000]{0:T(1024)(128)(4,1)}), s8[4194304]{0:T(1024)(128)(4,1)S(1)}, s32[]{:S(2)}) async-start(s8[8192000]{0:T(1024)(128)(4,1)} %bitcast.78), calls=%async_computation | async-start | bytes 8388608 | tf_op jit(solution)/shard_map/while
  77.5 8.6 %slice-start.1 = ((s8[8192000]{0:T(1024)(128)(4,1)}), s8[3997696]{0:T(1024)(128)(4,1)S(1)}, s32[]{:S(2)}) async-start(s8[8192000]{0:T(1024)(128)(4,1)} %bitcast.78), calls=%async_computation.1 | async-start | bytes 7995392 | tf_op jit(solution)/shard_map/while
  77.5 8.6 %copy-start = (bf16[300,528]{1,0:T(8,128)(2,1)S(1)}, bf16[300,528]{1,0:T(8,128)(2,1)}, u32[]{:S(2)}) copy-start(bf16[300,528]{1,0:T(8,128)(2,1)} %get-tuple-element.267.refs_8_.eig_ref) | copy-start | bytes 950404 | tf_op jit(solution)/shard_map/while
  77.5 8.6 %copy-start.1 = (bf16[16,528]{1,0:T(8,128)(2,1)S(1)}, bf16[16,528]{1,0:T(8,128)(2,1)}, u32[]{:S(2)}) copy-start(bf16[16,528]{1,0:T(8,128)(2,1)} %get-tuple-element.264.refs_4_) | copy-start | bytes 50692 | tf_op jit(solution)/shard_map/while
  77.5 8.6 %copy-start.2 = (bf16[528]{0:T(1024)(128)(2,1)S(1)}, bf16[528]{0:T(1024)(128)(2,1)}, u32[]{:S(2)}) copy-start(bf16[528]{0:T(1024)(128)(2,1)} %get-tuple-element.265.refs_6_) | copy-start | bytes 3172 | tf_op jit(solution)/shard_map/while
  77.5 8.6 %copy-start.3 = (bf16[528]{0:T(1024)(128)(2,1)S(1)}, bf16[528]{0:T(1024)(128)(2,1)}, u32[]{:S(2)}) copy-start(bf16[528]{0:T(1024)(128)(2,1)} %get-tuple-element.266.refs_7_) | copy-start | bytes 3172 | tf_op jit(solution)/shard_map/while
  77.5 7.1 %collective-permute-start.4 = (bf16[4,400]{1,0:T(4,128)(2,1)S(1)}, bf16[4,400]{1,0:T(4,128)(2,1)S(1)}, u32[]{:S(2)}, u32[]{:S(2)}) collective-permute-start(bf16[4,400]{1,0:T(4,128)(2,1)S(1)} %pad_maximum_fusion.13.refs_0_), channel_id=1, source_target_pairs={{0,32},{16,48},{32,64},{48,80},{64,96},{80,112},{96,0},{112,16},{1... | collective-permute-start | bytes 9608 | tf_op jit(solution)/shard_map/while/body/eval_jaxpr/ppermute | solution.py:320
  79.3 5.4 %collective-permute-start.3 = (bf16[4,400]{1,0:T(4,128)(2,1)S(1)}, bf16[4,400]{1,0:T(4,128)(2,1)S(1)}, u32[]{:S(2)}, u32[]{:S(2)}) collective-permute-start(bf16[4,400]{1,0:T(4,128)(2,1)S(1)} %pad_maximum_fusion.13.refs_0_), channel_id=1, source_target_pairs={{0,64},{16,80},{32,96},{48,112},{64,0},{80,16},{96,32},{112,48},{1... | collective-permute-start | bytes 9608 | tf_op jit(solution)/shard_map/while/body/eval_jaxpr/ppermute | solution.py:320
  82.4 3.6 %collective-permute-start.2 = (bf16[4,400]{1,0:T(4,128)(2,1)S(1)}, bf16[4,400]{1,0:T(4,128)(2,1)S(1)}, u32[]{:S(2)}, u32[]{:S(2)}) collective-permute-start(bf16[4,400]{1,0:T(4,128)(2,1)S(1)} %pad_maximum_fusion.13.refs_0_), channel_id=1, source_target_pairs={{0,96},{16,112},{32,0},{48,16},{64,32},{80,48},{96,64},{112,80},{1... | collective-permute-start | bytes 9608 | tf_op jit(solution)/shard_map/while/body/eval_jaxpr/ppermute | solution.py:320
  89.1 2.7 %collective-permute-start.5 = (f32[2,960,128]{2,1,0:T(8,128)S(1)}, f32[2,960,128]{2,1,0:T(8,128)S(1)}, u32[]{:S(2)}, u32[]{:S(2)}) collective-permute-start(f32[2,960,128]{2,1,0:T(8,128)S(1)} %get-tuple-element.214), channel_id=1, source_target_pairs={{0,16},{16,0},{32,48},{48,32},{64,80},{80,64},{96,112},{112,96},{1... | collective-permute-start | bytes 2949128 | tf_op jit(solution)/shard_map/while/body/eval_jaxpr/ppermute | solution.py:314
  90.7 8.2 %collective-permute-start.10 = (f32[2,960,128]{2,1,0:T(8,128)S(1)}, f32[2,960,128]{2,1,0:T(8,128)S(1)}, u32[]{:S(2)}, u32[]{:S(2)}) collective-permute-start(f32[2,960,128]{2,1,0:T(8,128)S(1)} %get-tuple-element.224), channel_id=1, source_target_pairs={{0,16},{16,0},{32,48},{48,32},{64,80},{80,64},{96,112},{112,96},{1... | collective-permute-start | bytes 2949128 | tf_op jit(solution)/shard_map/while/body/eval_jaxpr/ppermute | solution.py:314
  91.8 9.3 %collective-permute-start.11 = (bf16[960,128]{1,0:T(8,128)(2,1)S(1)}, bf16[960,128]{1,0:T(8,128)(2,1)S(1)}, u32[]{:S(2)}, u32[]{:S(2)}) collective-permute-start(bf16[960,128]{1,0:T(8,128)(2,1)S(1)} %get-tuple-element.216), channel_id=1, source_target_pairs={{0,32},{16,48},{32,64},{48,80},{64,96},{80,112},{96,0},{112,16},{1... | collective-permute-start | bytes 737288 | tf_op jit(solution)/shard_map/while/body/eval_jaxpr/ppermute | solution.py:320
  92.1 9.6 %collective-permute-start.8 = (bf16[960,128]{1,0:T(8,128)(2,1)S(1)}, bf16[960,128]{1,0:T(8,128)(2,1)S(1)}, u32[]{:S(2)}, u32[]{:S(2)}) collective-permute-start(bf16[960,128]{1,0:T(8,128)(2,1)S(1)} %get-tuple-element.217), channel_id=1, source_target_pairs={{0,96},{16,112},{32,0},{48,16},{64,32},{80,48},{96,64},{112,80},{1... | collective-permute-start | bytes 737288 | tf_op jit(solution)/shard_map/while/body/eval_jaxpr/ppermute | solution.py:320
  96.6 24.2 %copy-start.4 = (f32[1,400]{1,0:T(1,128)S(1)}, f32[1,400]{1,0:T(1,128)}, u32[]{:S(2)}) copy-start(f32[1,400]{1,0:T(1,128)} %get-tuple-element.269.prec_ref) | copy-start | bytes 4804 | tf_op jit(solution)/shard_map/while
  96.6 24.2 %copy-start.5 = (f32[300]{0:T(512)S(1)}, f32[300]{0:T(512)}, u32[]{:S(2)}) copy-start(f32[300]{0:T(512)} %get-tuple-element.270.weight_ref) | copy-start | bytes 3604 | tf_op jit(solution)/shard_map/while
  96.7 5.1 %collective-permute-start.7 = (f32[2,960,128]{2,1,0:T(8,128)S(1)}, f32[2,960,128]{2,1,0:T(8,128)S(1)}, u32[]{:S(2)}, u32[]{:S(2)}) collective-permute-start(f32[2,960,128]{2,1,0:T(8,128)S(1)} %get-tuple-element.223), channel_id=1, source_target_pairs={{0,16},{16,0},{32,48},{48,32},{64,80},{80,64},{96,112},{112,96},{1... | collective-permute-start | bytes 2949128 | tf_op jit(solution)/shard_map/while/body/eval_jaxpr/ppermute | solution.py:314
  98.3 28.1 %copy-start.6 = (f32[1,400]{1,0:T(1,128)S(1)}, f32[1,400]{1,0:T(1,128)}, u32[]{:S(2)}) copy-start(f32[1,400]{1,0:T(1,128)} %get-tuple-element.271.mean_ref) | copy-start | bytes 4804 | tf_op jit(solution)/shard_map/while
  98.3 12.1 %collective-permute-start.6 = (f32[2,960,128]{2,1,0:T(8,128)S(1)}, f32[2,960,128]{2,1,0:T(8,128)S(1)}, u32[]{:S(2)}, u32[]{:S(2)}) collective-permute-start(f32[2,960,128]{2,1,0:T(8,128)S(1)} %get-tuple-element.221), channel_id=1, source_target_pairs={{0,16},{16,0},{32,48},{48,32},{64,80},{80,64},{96,112},{112,96},{1... | collective-permute-start | bytes 2949128 | tf_op jit(solution)/shard_map/while/body/eval_jaxpr/ppermute | solution.py:314
  101.2 9.2 %collective-permute-start.15 = (bf16[2,400,128]{2,1,0:T(8,128)(2,1)S(1)}, bf16[2,400,128]{2,1,0:T(8,128)(2,1)S(1)}, u32[]{:S(2)}, u32[]{:S(2)}) collective-permute-start(bf16[2,400,128]{2,1,0:T(8,128)(2,1)S(1)} %pad_maximum_fusion.17), channel_id=1, source_target_pairs={{0,32},{16,48},{32,64},{48,80},{64,96},{80,112},{96,0},{112,16},{1... | collective-permute-start | bytes 614408 | tf_op jit(solution)/shard_map/while/body/eval_jaxpr/ppermute | solution.py:320
  101.4 14.5 %collective-permute-start.12 = (bf16[2,560,128]{2,1,0:T(8,128)(2,1)S(1)}, bf16[2,560,128]{2,1,0:T(8,128)(2,1)S(1)}, u32[]{:S(2)}, u32[]{:S(2)}) collective-permute-start(bf16[2,560,128]{2,1,0:T(8,128)(2,1)S(1)} %pad_maximum_fusion.15), channel_id=1, source_target_pairs={{0,32},{16,48},{32,64},{48,80},{64,96},{80,112},{96,0},{112,16},{1... | collective-permute-start | bytes 860168 | tf_op jit(solution)/shard_map/while/body/eval_jaxpr/ppermute | solution.py:320
  101.9 8.6 %collective-permute-start.14 = (bf16[2,400,128]{2,1,0:T(8,128)(2,1)S(1)}, bf16[2,400,128]{2,1,0:T(8,128)(2,1)S(1)}, u32[]{:S(2)}, u32[]{:S(2)}) collective-permute-start(bf16[2,400,128]{2,1,0:T(8,128)(2,1)S(1)} %pad_maximum_fusion.16), channel_id=1, source_target_pairs={{0,96},{16,112},{32,0},{48,16},{64,32},{80,48},{96,64},{112,80},{1... | collective-permute-start | bytes 614408 | tf_op jit(solution)/shard_map/while/body/eval_jaxpr/ppermute | solution.py:320
  105.0 10.9 %collective-permute-start.9 = (bf16[2,560,128]{2,1,0:T(8,128)(2,1)S(1)}, bf16[2,560,128]{2,1,0:T(8,128)(2,1)S(1)}, u32[]{:S(2)}, u32[]{:S(2)}) collective-permute-start(bf16[2,560,128]{2,1,0:T(8,128)(2,1)S(1)} %pad_maximum_fusion.14), channel_id=1, source_target_pairs={{0,96},{16,112},{32,0},{48,16},{64,32},{80,48},{96,64},{112,80},{1... | collective-permute-start | bytes 860168 | tf_op jit(solution)/shard_map/while/body/eval_jaxpr/ppermute | solution.py:320
  110.5 10.4 %collective-permute-start.16 = (bf16[400,128]{1,0:T(8,128)(2,1)S(1)}, bf16[400,128]{1,0:T(8,128)(2,1)S(1)}, u32[]{:S(2)}, u32[]{:S(2)}) collective-permute-start(bf16[400,128]{1,0:T(8,128)(2,1)S(1)} %get-tuple-element.229), channel_id=1, source_target_pairs={{0,128},{16,144},{32,160},{48,176},{64,192},{80,208},{96,224},{112... | collective-permute-start | bytes 307208 | tf_op jit(solution)/shard_map/while/body/eval_jaxpr/ppermute | solution.py:326
  116.0 10.4 %collective-permute-start.13 = (bf16[560,128]{1,0:T(8,128)(2,1)S(1)}, bf16[560,128]{1,0:T(8,128)(2,1)S(1)}, u32[]{:S(2)}, u32[]{:S(2)}) collective-permute-start(bf16[560,128]{1,0:T(8,128)(2,1)S(1)} %get-tuple-element.227), channel_id=1, source_target_pairs={{0,128},{16,144},{32,160},{48,176},{64,192},{80,208},{96,224},{112... | collective-permute-start | bytes 430088 | tf_op jit(solution)/shard_map/while/body/eval_jaxpr/ppermute | solution.py:326
  (4 other events, 32.8 us)

commit v2 on v1

--- a/solution.py
+++ b/solution.py
@@ -264,13 +264,15 @@
     v = [block[first + i : first + i + 1] + block[first + 3 + i : first + 4 + i] for i in range(3)]
     v0 = jnp.broadcast_to(v[0], (8, 128))
     v12 = jnp.broadcast_to(jnp.concatenate(v[1:], axis=1)[:, :LOW], (8, LOW))
-    shift = wide(root * (state_ref[...] - mean_ref[...]), 512)
+    shift = wide(root, 512) * (state_ref[...] - wide(mean_ref[...], 512))
     shift = jnp.broadcast_to(shift, (8, 512))
-    v0 -= dot_nt(shift, top)
-    v12 -= dot_nt(shift, low)
-    s10 = dot_nt(low, top)
+    both = jnp.concatenate([low, shift], axis=0)
+    by_top, by_low = dot_nt(both, top), dot_nt(both, low)
+    v0 -= by_top[LOW:]
+    v12 -= by_low[LOW:]
+    s10 = by_top[:LOW]
     t10 = dot_nn(s10, inv0)
-    s = plus_diagonal(dot_nt(low, low), noise) - dot_nt(t10, s10)
+    s = plus_diagonal(by_low[:LOW], noise) - dot_nt(t10, s10)
     v12 -= dot_nt(v0, t10)
     inv1 = spd_inverse(tiles_of(s[:128, :128]))
     s21 = s[128:, :128]
@@ -285,20 +287,21 @@
     y12 = jnp.concatenate([y1, y2], axis=1)
     y0 = dot_nn(v0 - dot_nn(y12, s10), inv0)
     step = (dot_nn(y0, top) + dot_nn(y12, low)) * scale
-    new = mean_ref[...] - step[0:1, : mean_ref.shape[1]]
+    new = wide(mean_ref[...], 512) - step[0:1]
     out_ref[...] = new
-    short_ref[...] = new.astype(bf16)
+    short_ref[...] = new[:, : mean_ref.shape[1]].astype(bf16)
 
 
 def low_step(keep, got, top, inv0, state, prec, mean, weight):
     return pl.pallas_call(
         low_kernel,
         out_shape=(
-            jax.ShapeDtypeStruct(mean.shape, f32),
+            jax.ShapeDtypeStruct(state.shape, f32),
             jax.ShapeDtypeStruct(mean.shape, bf16),
         ),
         cost_estimate=pl.CostEstimate(flops=10**9, bytes_accessed=0, transcendentals=0),
         compiler_params=GRANT,
+        input_output_aliases={4: 0},
         name="low_step",
     )(keep, got, top, inv0, state, prec, mean, weight)
 
@@ -369,12 +372,13 @@
         later = after(slope, *relay)
         behind = chip_sum(3, later)
         own = chip_sum(0, after(later, behind[0]))
-        both = []
+        both, gate = [], later
         for part in (slice(0, CUT), slice(CUT, BLOCK)):
             up = [chunk(ahead, part, 0) + forth[part].astype(f32), chunk(ahead, part, 1)]
             down = [chunk(behind, part, 0), chunk(behind, part, 1) + back[part].astype(f32)]
-            up = move_y(jnp.stack(up).astype(bf16), 1)
-            down = move_y(jnp.stack(down).astype(bf16), -1)
+            up = after(jnp.stack(up).astype(bf16), gate)
+            down = gate = jnp.stack(down).astype(bf16)
+            up, down = move_y(up, 1), move_y(down, -1)
             near = [
                 chunk(own, part, dz) + up[dz].astype(f32) + down[dz].astype(f32)
                 for dz in range(2)
@@ -383,7 +387,9 @@
         top, inv0 = top_step(*both[0], prec, pc_weight)
         return low_step(*both[1], top, inv0, state, prec, prior_mean, pc_weight)
 
-    return lax.fori_loop(0, ITERS, iterate, (state0, state0.astype(bf16)))[0]
+    count = state0.shape[1]
+    start = (jnp.pad(state0, ((0, 0), (0, 512 - count))), state0.astype(bf16))
+    return lax.fori_loop(0, ITERS, iterate, start)[0][:, :count]
 
 
 def solution(mesh):

time: 136 us -> 133 us (0.978)
  Pallas kernels: 41.5 us -> 39.3 us
  starting transfers between devices: 65.4 us -> 66.9 us
    pallas_call x2, Pallas kernels: 16.9 us -> 14.7 us  [low_step(): pl.pallas_call(low_kernel, out_shape=(jax.ShapeDtypeStruct(state.shape, f...]
    ppermute x18, waiting for transfers between devices: 14 us -> 12.5 us  [move_y(): lax.ppermute(value, 'chan', [(index_of(z, y, c), index_of(z, (y + step) %...]
    while x38 -> x36, local copies, waits for them, and re-layouts: 1.47 us -> 0.11 us
  transfers between devices with their start and end apart: 34 -> 34, of which waited for: 14 -> 15; matrix products, arithmetic and copies ran while one was open for 2% -> 1% of each run, Pallas kernels for 14% -> 14%
where the time goes in v2:
time: 133 us
  starting transfers between devices  66.9 us (50%)
  Pallas kernels  39.3 us (30%)
  waiting for transfers between devices  22.3 us (17%)
  other arithmetic  2.06 us (2%)
  local copies, waits for them, and re-layouts  1.39 us (1%)
    ppermute x6, starting transfers between devices, swap_z(): lax.ppermute(value, 'chan', [(index_of(z, y, c), index_of(1 - z, y, c)) f...  33.4 us
    ppermute x18, starting transfers between devices, move_y(): lax.ppermute(value, 'chan', [(index_of(z, y, c), index_of(z, (y + step) %...  30.8 us
    pallas_call x2, Pallas kernels, low_step(): pl.pallas_call(low_kernel, out_shape=(jax.ShapeDtypeStruct(state.shape, f...  14.7 us
    ppermute x18, waiting for transfers between devices, move_y(): lax.ppermute(value, 'chan', [(index_of(z, y, c), index_of(z, (y + step) %...  12.5 us
    pallas_call x8, Pallas kernels, project(): pl.pallas_call(functools.partial(project_kernel, dy), out_shape=(jax.Shap...  12 us
    pallas_call x2, Pallas kernels, top_step(): pl.pallas_call(top_kernel, out_shape=(jax.ShapeDtypeStruct((TOP, 512), f3...  8.06 us
    ppermute x6, waiting for transfers between devices, swap_z(): lax.ppermute(value, 'chan', [(index_of(z, y, c), index_of(1 - z, y, c)) f...  6.53 us
    ppermute x10, waiting for transfers between devices, swap_core(): lax.ppermute(value, 'chan', [(index_of(z, y, c), index_of(z, y, 1 - c)) f...  3.28 us
  transfers between devices with their start and end apart: 34, of which 15 were waited for; matrix products, arithmetic and copies ran while one was open for 1% of the time, Pallas kernels for 14%

profile of v2, /device:TPU:2, one launch (start us, length us, event | category | flops | bytes accessed | tf_op | source)
XLA Modules:
  0.0 132.5 jit_solution(14688035014335691198)
XLA Ops:
  0.0 0.7 convert_element_type.77
  0.7 0.7 pad.4
  1.4 130.6 %while.12 = (s32[]{:T(128)}, f32[1,512]{1,0:T(1,128)S(1)}, bf16[1,400]{1,0:T(2,128)(2,1)S(1)}, s32[16,16]{1,0:T(8,128)}, bf16[16,528]{1,0:T(8,128)(2,1)}, /*inde...) while((s32[]{:T(128)}, f32[1,512]{1,0:T(1,128)S(1)}, ...), condition=%wide.region_1.2_spmd, body=%wide.region_0.1_spmd.sunk | while | flops 27003817984 | bytes 62122200 | solution.py:392
  1.4 1.2 collective-permute-done
  2.6 7.3 %collective-permute-start.1 = (bf16[2,400]{1,0:T(2,128)(2,1)S(1)}, bf16[2,400]{1,0:T(2,128)(2,1)S(1)}, u32[]{:S(2)}, u32[]{:S(2)}) collective-permute-start(bf16[2,400]{1,0:T(2,128)(2,1)S(1)} %pad_maximum_fusion.12), channel_id=1, source_target_pairs={{0,128},{16,144},{32,160},{48,176},{64,192},{80,208},{96,224},{112... | collective-permute-start | bytes 4808 | tf_op jit(solution)/shard_map/while/body/eval_jaxpr/ppermute | solution.py:329
  9.8 1.6 %collective-permute-done.1 = bf16[2,400]{1,0:T(2,128)(2,1)S(1)} collective-permute-done((bf16[2,400]{1,0:T(2,128)(2,1)S(1)}, bf16[2,400]{1,0:T(2,128)(2,1)S(1)}, u32[]{:S(2)}, u32[]{:S(2)}) %collective-permute-start.1) | collective-permute-done | bytes 1632 | tf_op jit(solution)/shard_map/while/body/eval_jaxpr/ppermute | solution.py:329
  11.5 1.7 %collective-permute-start.4 = (bf16[4,400]{1,0:T(4,128)(2,1)S(1)}, bf16[4,400]{1,0:T(4,128)(2,1)S(1)}, u32[]{:S(2)}, u32[]{:S(2)}) collective-permute-start(bf16[4,400]{1,0:T(4,128)(2,1)S(1)} %pad_maximum_fusion.13.refs_0_), channel_id=1, source_target_pairs={{0,32},{16,48},{32,64},{48,80},{64,96},{80,112},{96,0},{112,16},{1... | collective-permute-start | bytes 9608 | tf_op jit(solution)/shard_map/while/body/eval_jaxpr/ppermute | solution.py:323
  13.1 2.9 %collective-permute-start.3 = (bf16[4,400]{1,0:T(4,128)(2,1)S(1)}, bf16[4,400]{1,0:T(4,128)(2,1)S(1)}, u32[]{:S(2)}, u32[]{:S(2)}) collective-permute-start(bf16[4,400]{1,0:T(4,128)(2,1)S(1)} %pad_maximum_fusion.13.refs_0_), channel_id=1, source_target_pairs={{0,64},{16,80},{32,96},{48,112},{64,0},{80,16},{96,32},{112,48},{1... | collective-permute-start | bytes 9608 | tf_op jit(solution)/shard_map/while/body/eval_jaxpr/ppermute | solution.py:323
  16.0 1.3 %collective-permute-start.2 = (bf16[4,400]{1,0:T(4,128)(2,1)S(1)}, bf16[4,400]{1,0:T(4,128)(2,1)S(1)}, u32[]{:S(2)}, u32[]{:S(2)}) collective-permute-start(bf16[4,400]{1,0:T(4,128)(2,1)S(1)} %pad_maximum_fusion.13.refs_0_), channel_id=1, source_target_pairs={{0,96},{16,112},{32,0},{48,16},{64,32},{80,48},{96,64},{112,80},{1... | collective-permute-start | bytes 9608 | tf_op jit(solution)/shard_map/while/body/eval_jaxpr/ppermute | solution.py:323
  17.4 0.8 valid_channels.1.refs_5_
  18.2 1.4 %collective-permute-done.2.refs_1_ = bf16[4,400]{1,0:T(4,128)(2,1)S(1)} collective-permute-done((bf16[4,400]{1,0:T(4,128)(2,1)S(1)}, bf16[4,400]{1,0:T(4,128)(2,1)S(1)}, u32[]{:S(2)}, u32[]{:S(2)}) %collective-permute-start.2) | collective-permute-done | bytes 3232 | tf_op jit(solution)/shard_map/while/body/eval_jaxpr/ppermute | solution.py:323
  19.7 1.4 %slopes.1 = (f32[16,528]{1,0:T(8,128)S(1)}, f32[16,384]{1,0:T(8,128)S(1)}) custom-call(bf16[4,400]{1,0:T(4,128)(2,1)S(1)} %pad_maximum_fusion.13.refs_0_, bf16[4,400]{1,0:T(4,128)(2,1)S(1)} %collective-permute-done.2.refs_1_, bf16[4,400]{1,0:T(4,128)(2,1)S(1)} %collective-permute-done.3.refs_2_, bf16[4,400]{1,0:T(4,128)(2,1)S(1)} %collective-permute-done.4.refs_3_, ...), custom_call_target="tpu_custom_call" | custom-call | flops 1000000000 | tf_op jit(solution)/shard_map/while/body/eval_jaxpr/slopes/pallas_call | solution.py:81
  21.1 1.5 %project.4 = (f32[2,960,128]{2,1,0:T(8,128)S(1)}, f32[2,960,128]{2,1,0:T(8,128)S(1)}) custom-call(f32[16,528]{1,0:T(8,128)S(1)} %get-tuple-element.224.slope_ref, f32[16,384]{1,0:T(8,128)S(1)} %get-tuple-element.217.resid_ref, bf16[300,528]{1,0:T(8,128)(2,1)S(1)} %copy-done, bf16[16,400,528]{2,1,0:T(8,128)(2,1)S(1)} %bitcast.80), custom_call_target="tpu_custom_call" | custom-call | flops 1000000000 | tf_op jit(solution)/shard_map/while/body/eval_jaxpr/project/pallas_call | solution.py:135
  22.8 1.5 %project.7 = (f32[2,960,128]{2,1,0:T(8,128)S(1)}, f32[2,960,128]{2,1,0:T(8,128)S(1)}) custom-call(f32[16,528]{1,0:T(8,128)S(1)} %get-tuple-element.224.slope_ref, f32[16,384]{1,0:T(8,128)S(1)} %get-tuple-element.217.resid_ref, bf16[300,528]{1,0:T(8,128)(2,1)S(1)} %copy-done, bf16[16,400,528]{2,1,0:T(8,128)(2,1)S(1)} %bitcast.80), custom_call_target="tpu_custom_call" | custom-call | flops 1000000000 | tf_op jit(solution)/shard_map/while/body/eval_jaxpr/project/pallas_call | solution.py:135
  25.7 3.0 %collective-permute-start.8 = (bf16[960,128]{1,0:T(8,128)(2,1)S(1)}, bf16[960,128]{1,0:T(8,128)(2,1)S(1)}, u32[]{:S(2)}, u32[]{:S(2)}) collective-permute-start(bf16[960,128]{1,0:T(8,128)(2,1)S(1)} %get-tuple-element.221), channel_id=1, source_target_pairs={{0,96},{16,112},{32,0},{48,16},{64,32},{80,48},{96,64},{112,80},{1... | collective-permute-start | bytes 737288 | tf_op jit(solution)/shard_map/while/body/eval_jaxpr/ppermute | solution.py:323
  28.7 1.5 %project.5 = (f32[2,960,128]{2,1,0:T(8,128)S(1)}, f32[2,960,128]{2,1,0:T(8,128)S(1)}) custom-call(f32[16,528]{1,0:T(8,128)S(1)} %get-tuple-element.224.slope_ref, f32[16,384]{1,0:T(8,128)S(1)} %get-tuple-element.217.resid_ref, bf16[300,528]{1,0:T(8,128)(2,1)S(1)} %copy-done, bf16[16,400,528]{2,1,0:T(8,128)(2,1)S(1)} %bitcast.80), custom_call_target="tpu_custom_call" | custom-call | flops 1000000000 | tf_op jit(solution)/shard_map/while/body/eval_jaxpr/project/pallas_call | solution.py:135
  30.3 1.5 %project.6 = (f32[2,960,128]{2,1,0:T(8,128)S(1)}, f32[2,960,128]{2,1,0:T(8,128)S(1)}) custom-call(f32[16,528]{1,0:T(8,128)S(1)} %get-tuple-element.224.slope_ref, f32[16,384]{1,0:T(8,128)S(1)} %get-tuple-element.217.resid_ref, bf16[300,528]{1,0:T(8,128)(2,1)S(1)} %copy-done, bf16[16,400,528]{2,1,0:T(8,128)(2,1)S(1)} %bitcast.80), custom_call_target="tpu_custom_call" | custom-call | flops 1000000000 | tf_op jit(solution)/shard_map/while/body/eval_jaxpr/project/pallas_call | solution.py:135
  32.5 2.2 %collective-permute-done.11 = bf16[960,128]{1,0:T(8,128)(2,1)S(1)} collective-permute-done((bf16[960,128]{1,0:T(8,128)(2,1)S(1)}, bf16[960,128]{1,0:T(8,128)(2,1)S(1)}, u32[]{:S(2)}, u32[]{:S(2)}) %collective-permute-start.11) | collective-permute-done | bytes 245792 | tf_op jit(solution)/shard_map/while/body/eval_jaxpr/ppermute | solution.py:323
  35.1 3.3 %collective-permute-start.14 = (bf16[2,400,128]{2,1,0:T(8,128)(2,1)S(1)}, bf16[2,400,128]{2,1,0:T(8,128)(2,1)S(1)}, u32[]{:S(2)}, u32[]{:S(2)}) collective-permute-start(bf16[2,400,128]{2,1,0:T(8,128)(2,1)S(1)} %pad_maximum_fusion.16), channel_id=1, source_target_pairs={{0,96},{16,112},{32,0},{48,16},{64,32},{80,48},{96,64},{112,80},{1... | collective-permute-start | bytes 614408 | tf_op jit(solution)/shard_map/while/body/eval_jaxpr/ppermute | solution.py:323
  38.5 3.3 %collective-permute-start.9 = (bf16[2,560,128]{2,1,0:T(8,128)(2,1)S(1)}, bf16[2,560,128]{2,1,0:T(8,128)(2,1)S(1)}, u32[]{:S(2)}, u32[]{:S(2)}) collective-permute-start(bf16[2,560,128]{2,1,0:T(8,128)(2,1)S(1)} %pad_maximum_fusion.14), channel_id=1, source_target_pairs={{0,96},{16,112},{32,0},{48,16},{64,32},{80,48},{96,64},{112,80},{1... | collective-permute-start | bytes 860168 | tf_op jit(solution)/shard_map/while/body/eval_jaxpr/ppermute | solution.py:323
  41.8 1.9 %collective-permute-done.15 = bf16[2,400,128]{2,1,0:T(8,128)(2,1)S(1)} collective-permute-done((bf16[2,400,128]{2,1,0:T(8,128)(2,1)S(1)}, bf16[2,400,128]{2,1,0:T(8,128)(2,1)S(1)}, u32[]{:S(2)}, u32[]{:S(2)}) %collective-permute-start.15) | collective-permute-done | bytes 204832 | tf_op jit(solution)/shard_map/while/body/eval_jaxpr/ppermute | solution.py:323
  43.8 6.0 %collective-permute-start.16 = (bf16[400,128]{1,0:T(8,128)(2,1)S(1)}, bf16[400,128]{1,0:T(8,128)(2,1)S(1)}, u32[]{:S(2)}, u32[]{:S(2)}) collective-permute-start(bf16[400,128]{1,0:T(8,128)(2,1)S(1)} %get-tuple-element.235), channel_id=1, source_target_pairs={{0,128},{16,144},{32,160},{48,176},{64,192},{80,208},{96,224},{112... | collective-permute-start | bytes 307208 | tf_op jit(solution)/shard_map/while/body/eval_jaxpr/ppermute | solution.py:329
  50.0 4.6 %collective-permute-start.13 = (bf16[560,128]{1,0:T(8,128)(2,1)S(1)}, bf16[560,128]{1,0:T(8,128)(2,1)S(1)}, u32[]{:S(2)}, u32[]{:S(2)}) collective-permute-start(bf16[560,128]{1,0:T(8,128)(2,1)S(1)} %get-tuple-element.232), channel_id=1, source_target_pairs={{0,128},{16,144},{32,160},{48,176},{64,192},{80,208},{96,224},{112... | collective-permute-start | bytes 430088 | tf_op jit(solution)/shard_map/while/body/eval_jaxpr/ppermute | solution.py:329
  54.6 4.0 %top_step.1 = (f32[128,512]{1,0:T(8,128)S(1)}, f32[128,128]{1,0:T(8,128)S(1)}) custom-call(f32[400,128]{1,0:T(8,128)S(1)} %get-tuple-element.234.keep_ref, bf16[400,128]{1,0:T(8,128)(2,1)S(1)} %collective-permute-done.16.got_ref, f32[1,400]{1,0:T(1,128)S(1)} %copy-done.5, f32[300]{0:T(512)S(1)} %copy-done.6), custom_call_target="tpu_custom_call" | custom-call | flops 1000000000 | tf_op jit(solution)/shard_map/while/body/eval_jaxpr/top_step/pallas_call | solution.py:241
  58.6 1.3 collective-permute-done.13.got_ref
  59.9 7.3 %low_step.1 = (f32[1,512]{1,0:T(1,128)S(1)}, bf16[1,400]{1,0:T(2,128)(2,1)S(1)}) custom-call(f32[560,128]{1,0:T(8,128)S(1)} %get-tuple-element.231.keep_ref, bf16[560,128]{1,0:T(8,128)(2,1)S(1)} %collective-permute-done.13.got_ref, f32[128,512]{1,0:T(8,128)S(1)} %get-tuple-element.236.top_ref, ...), custom_call_target="tpu_custom_call", output_to_operand_aliasing={{0}: (4, {})} | custom-call | flops 1000000000 | tf_op jit(solution)/shard_map/while/body/eval_jaxpr/low_step/pallas_call | solution.py:296
  67.3 1.1 collective-permute-done
  68.5 5.5 %collective-permute-start.1 = (bf16[2,400]{1,0:T(2,128)(2,1)S(1)}, bf16[2,400]{1,0:T(2,128)(2,1)S(1)}, u32[]{:S(2)}, u32[]{:S(2)}) collective-permute-start(bf16[2,400]{1,0:T(2,128)(2,1)S(1)} %pad_maximum_fusion.12), channel_id=1, source_target_pairs={{0,128},{16,144},{32,160},{48,176},{64,192},{80,208},{96,224},{112... | collective-permute-start | bytes 4808 | tf_op jit(solution)/shard_map/while/body/eval_jaxpr/ppermute | solution.py:329
  74.0 2.1 %collective-permute-done.1 = bf16[2,400]{1,0:T(2,128)(2,1)S(1)} collective-permute-done((bf16[2,400]{1,0:T(2,128)(2,1)S(1)}, bf16[2,400]{1,0:T(2,128)(2,1)S(1)}, u32[]{:S(2)}, u32[]{:S(2)}) %collective-permute-start.1) | collective-permute-done | bytes 1632 | tf_op jit(solution)/shard_map/while/body/eval_jaxpr/ppermute | solution.py:329
  76.2 4.8 %collective-permute-start.3 = (bf16[4,400]{1,0:T(4,128)(2,1)S(1)}, bf16[4,400]{1,0:T(4,128)(2,1)S(1)}, u32[]{:S(2)}, u32[]{:S(2)}) collective-permute-start(bf16[4,400]{1,0:T(4,128)(2,1)S(1)} %pad_maximum_fusion.13.refs_0_), channel_id=1, source_target_pairs={{0,64},{16,80},{32,96},{48,112},{64,0},{80,16},{96,32},{112,48},{1... | collective-permute-start | bytes 9608 | tf_op jit(solution)/shard_map/while/body/eval_jaxpr/ppermute | solution.py:323
  81.0 0.8 valid_channels.1.refs_5_
  81.9 0.8 collective-permute-done.3.refs_2_
  82.6 2.0 %collective-permute-done.2.refs_1_ = bf16[4,400]{1,0:T(4,128)(2,1)S(1)} collective-permute-done((bf16[4,400]{1,0:T(4,128)(2,1)S(1)}, bf16[4,400]{1,0:T(4,128)(2,1)S(1)}, u32[]{:S(2)}, u32[]{:S(2)}) %collective-permute-start.2) | collective-permute-done | bytes 3232 | tf_op jit(solution)/shard_map/while/body/eval_jaxpr/ppermute | solution.py:323
  84.7 1.4 %slopes.1 = (f32[16,528]{1,0:T(8,128)S(1)}, f32[16,384]{1,0:T(8,128)S(1)}) custom-call(bf16[4,400]{1,0:T(4,128)(2,1)S(1)} %pad_maximum_fusion.13.refs_0_, bf16[4,400]{1,0:T(4,128)(2,1)S(1)} %collective-permute-done.2.refs_1_, bf16[4,400]{1,0:T(4,128)(2,1)S(1)} %collective-permute-done.3.refs_2_, bf16[4,400]{1,0:T(4,128)(2,1)S(1)} %collective-permute-done.4.refs_3_, ...), custom_call_target="tpu_custom_call" | custom-call | flops 1000000000 | tf_op jit(solution)/shard_map/while/body/eval_jaxpr/slopes/pallas_call | solution.py:81
  86.1 1.5 %project.4 = (f32[2,960,128]{2,1,0:T(8,128)S(1)}, f32[2,960,128]{2,1,0:T(8,128)S(1)}) custom-call(f32[16,528]{1,0:T(8,128)S(1)} %get-tuple-element.224.slope_ref, f32[16,384]{1,0:T(8,128)S(1)} %get-tuple-element.217.resid_ref, bf16[300,528]{1,0:T(8,128)(2,1)S(1)} %copy-done, bf16[16,400,528]{2,1,0:T(8,128)(2,1)S(1)} %bitcast.80), custom_call_target="tpu_custom_call" | custom-call | flops 1000000000 | tf_op jit(solution)/shard_map/while/body/eval_jaxpr/project/pallas_call | solution.py:135
  87.8 1.5 %project.7 = (f32[2,960,128]{2,1,0:T(8,128)S(1)}, f32[2,960,128]{2,1,0:T(8,128)S(1)}) custom-call(f32[16,528]{1,0:T(8,128)S(1)} %get-tuple-element.224.slope_ref, f32[16,384]{1,0:T(8,128)S(1)} %get-tuple-element.217.resid_ref, bf16[300,528]{1,0:T(8,128)(2,1)S(1)} %copy-done, bf16[16,400,528]{2,1,0:T(8,128)(2,1)S(1)} %bitcast.80), custom_call_target="tpu_custom_call" | custom-call | flops 1000000000 | tf_op jit(solution)/shard_map/while/body/eval_jaxpr/project/pallas_call | solution.py:135
  90.5 3.2 %collective-permute-start.8 = (bf16[960,128]{1,0:T(8,128)(2,1)S(1)}, bf16[960,128]{1,0:T(8,128)(2,1)S(1)}, u32[]{:S(2)}, u32[]{:S(2)}) collective-permute-start(bf16[960,128]{1,0:T(8,128)(2,1)S(1)} %get-tuple-element.221), channel_id=1, source_target_pairs={{0,96},{16,112},{32,0},{48,16},{64,32},{80,48},{96,64},{112,80},{1... | collective-permute-start | bytes 737288 | tf_op jit(solution)/shard_map/while/body/eval_jaxpr/ppermute | solution.py:323
  93.7 1.5 %project.5 = (f32[2,960,128]{2,1,0:T(8,128)S(1)}, f32[2,960,128]{2,1,0:T(8,128)S(1)}) custom-call(f32[16,528]{1,0:T(8,128)S(1)} %get-tuple-element.224.slope_ref, f32[16,384]{1,0:T(8,128)S(1)} %get-tuple-element.217.resid_ref, bf16[300,528]{1,0:T(8,128)(2,1)S(1)} %copy-done, bf16[16,400,528]{2,1,0:T(8,128)(2,1)S(1)} %bitcast.80), custom_call_target="tpu_custom_call" | custom-call | flops 1000000000 | tf_op jit(solution)/shard_map/while/body/eval_jaxpr/project/pallas_call | solution.py:135
  95.3 1.5 %project.6 = (f32[2,960,128]{2,1,0:T(8,128)S(1)}, f32[2,960,128]{2,1,0:T(8,128)S(1)}) custom-call(f32[16,528]{1,0:T(8,128)S(1)} %get-tuple-element.224.slope_ref, f32[16,384]{1,0:T(8,128)S(1)} %get-tuple-element.217.resid_ref, bf16[300,528]{1,0:T(8,128)(2,1)S(1)} %copy-done, bf16[16,400,528]{2,1,0:T(8,128)(2,1)S(1)} %bitcast.80), custom_call_target="tpu_custom_call" | custom-call | flops 1000000000 | tf_op jit(solution)/shard_map/while/body/eval_jaxpr/project/pallas_call | solution.py:135
  97.5 2.2 %collective-permute-done.11 = bf16[960,128]{1,0:T(8,128)(2,1)S(1)} collective-permute-done((bf16[960,128]{1,0:T(8,128)(2,1)S(1)}, bf16[960,128]{1,0:T(8,128)(2,1)S(1)}, u32[]{:S(2)}, u32[]{:S(2)}) %collective-permute-start.11) | collective-permute-done | bytes 245792 | tf_op jit(solution)/shard_map/while/body/eval_jaxpr/ppermute | solution.py:323
  100.1 3.3 %collective-permute-start.14 = (bf16[2,400,128]{2,1,0:T(8,128)(2,1)S(1)}, bf16[2,400,128]{2,1,0:T(8,128)(2,1)S(1)}, u32[]{:S(2)}, u32[]{:S(2)}) collective-permute-start(bf16[2,400,128]{2,1,0:T(8,128)(2,1)S(1)} %pad_maximum_fusion.16), channel_id=1, source_target_pairs={{0,96},{16,112},{32,0},{48,16},{64,32},{80,48},{96,64},{112,80},{1... | collective-permute-start | bytes 614408 | tf_op jit(solution)/shard_map/while/body/eval_jaxpr/ppermute | solution.py:323
  103.5 3.3 %collective-permute-start.9 = (bf16[2,560,128]{2,1,0:T(8,128)(2,1)S(1)}, bf16[2,560,128]{2,1,0:T(8,128)(2,1)S(1)}, u32[]{:S(2)}, u32[]{:S(2)}) collective-permute-start(bf16[2,560,128]{2,1,0:T(8,128)(2,1)S(1)} %pad_maximum_fusion.14), channel_id=1, source_target_pairs={{0,96},{16,112},{32,0},{48,16},{64,32},{80,48},{96,64},{112,80},{1... | collective-permute-start | bytes 860168 | tf_op jit(solution)/shard_map/while/body/eval_jaxpr/ppermute | solution.py:323
  106.8 1.9 %collective-permute-done.15 = bf16[2,400,128]{2,1,0:T(8,128)(2,1)S(1)} collective-permute-done((bf16[2,400,128]{2,1,0:T(8,128)(2,1)S(1)}, bf16[2,400,128]{2,1,0:T(8,128)(2,1)S(1)}, u32[]{:S(2)}, u32[]{:S(2)}) %collective-permute-start.15) | collective-permute-done | bytes 204832 | tf_op jit(solution)/shard_map/while/body/eval_jaxpr/ppermute | solution.py:323
  108.8 5.4 %collective-permute-start.16 = (bf16[400,128]{1,0:T(8,128)(2,1)S(1)}, bf16[400,128]{1,0:T(8,128)(2,1)S(1)}, u32[]{:S(2)}, u32[]{:S(2)}) collective-permute-start(bf16[400,128]{1,0:T(8,128)(2,1)S(1)} %get-tuple-element.235), channel_id=1, source_target_pairs={{0,128},{16,144},{32,160},{48,176},{64,192},{80,208},{96,224},{112... | collective-permute-start | bytes 307208 | tf_op jit(solution)/shard_map/while/body/eval_jaxpr/ppermute | solution.py:329
  114.3 4.6 %collective-permute-start.13 = (bf16[560,128]{1,0:T(8,128)(2,1)S(1)}, bf16[560,128]{1,0:T(8,128)(2,1)S(1)}, u32[]{:S(2)}, u32[]{:S(2)}) collective-permute-start(bf16[560,128]{1,0:T(8,128)(2,1)S(1)} %get-tuple-element.232), channel_id=1, source_target_pairs={{0,128},{16,144},{32,160},{48,176},{64,192},{80,208},{96,224},{112... | collective-permute-start | bytes 430088 | tf_op jit(solution)/shard_map/while/body/eval_jaxpr/ppermute | solution.py:329
  119.0 4.0 %top_step.1 = (f32[128,512]{1,0:T(8,128)S(1)}, f32[128,128]{1,0:T(8,128)S(1)}) custom-call(f32[400,128]{1,0:T(8,128)S(1)} %get-tuple-element.234.keep_ref, bf16[400,128]{1,0:T(8,128)(2,1)S(1)} %collective-permute-done.16.got_ref, f32[1,400]{1,0:T(1,128)S(1)} %copy-done.5, f32[300]{0:T(512)S(1)} %copy-done.6), custom_call_target="tpu_custom_call" | custom-call | flops 1000000000 | tf_op jit(solution)/shard_map/while/body/eval_jaxpr/top_step/pallas_call | solution.py:241
  123.0 1.6 %collective-permute-done.13.got_ref = bf16[560,128]{1,0:T(8,128)(2,1)S(1)} collective-permute-done((bf16[560,128]{1,0:T(8,128)(2,1)S(1)}, bf16[560,128]{1,0:T(8,128)(2,1)S(1)}, u32[]{:S(2)}, u32[]{:S(2)}) %collective-permute-start.13) | collective-permute-done | bytes 143392 | tf_op jit(solution)/shard_map/while/body/eval_jaxpr/ppermute | solution.py:329
  124.6 7.3 %low_step.1 = (f32[1,512]{1,0:T(1,128)S(1)}, bf16[1,400]{1,0:T(2,128)(2,1)S(1)}) custom-call(f32[560,128]{1,0:T(8,128)S(1)} %get-tuple-element.231.keep_ref, bf16[560,128]{1,0:T(8,128)(2,1)S(1)} %collective-permute-done.13.got_ref, f32[128,512]{1,0:T(8,128)S(1)} %get-tuple-element.236.top_ref, ...), custom_call_target="tpu_custom_call", output_to_operand_aliasing={{0}: (4, {})} | custom-call | flops 1000000000 | tf_op jit(solution)/shard_map/while/body/eval_jaxpr/low_step/pallas_call | solution.py:296
  (113 shorter events, 6.4 us)
Async XLA Ops:
  1.4 1.2 collective-permute-start
  2.6 8.8 %collective-permute-start.1 = (bf16[2,400]{1,0:T(2,128)(2,1)S(1)}, bf16[2,400]{1,0:T(2,128)(2,1)S(1)}, u32[]{:S(2)}, u32[]{:S(2)}) collective-permute-start(bf16[2,400]{1,0:T(2,128)(2,1)S(1)} %pad_maximum_fusion.12), channel_id=1, source_target_pairs={{0,128},{16,144},{32,160},{48,176},{64,192},{80,208},{96,224},{112... | collective-permute-start | bytes 4808 | tf_op jit(solution)/shard_map/while/body/eval_jaxpr/ppermute | solution.py:329
  11.4 8.2 %slice-start = ((s8[8192000]{0:T(1024)(128)(4,1)}), s8[4194304]{0:T(1024)(128)(4,1)S(1)}, s32[]{:S(2)}) async-start(s8[8192000]{0:T(1024)(128)(4,1)} %bitcast.79), calls=%async_computation | async-start | bytes 8388608 | tf_op jit(solution)/shard_map/while
  11.4 8.2 %slice-start.1 = ((s8[8192000]{0:T(1024)(128)(4,1)}), s8[3997696]{0:T(1024)(128)(4,1)S(1)}, s32[]{:S(2)}) async-start(s8[8192000]{0:T(1024)(128)(4,1)} %bitcast.79), calls=%async_computation.1 | async-start | bytes 7995392 | tf_op jit(solution)/shard_map/while
  11.5 6.7 %collective-permute-start.4 = (bf16[4,400]{1,0:T(4,128)(2,1)S(1)}, bf16[4,400]{1,0:T(4,128)(2,1)S(1)}, u32[]{:S(2)}, u32[]{:S(2)}) collective-permute-start(bf16[4,400]{1,0:T(4,128)(2,1)S(1)} %pad_maximum_fusion.13.refs_0_), channel_id=1, source_target_pairs={{0,32},{16,48},{32,64},{48,80},{64,96},{80,112},{96,0},{112,16},{1... | collective-permute-start | bytes 9608 | tf_op jit(solution)/shard_map/while/body/eval_jaxpr/ppermute | solution.py:323
  13.1 5.1 %collective-permute-start.3 = (bf16[4,400]{1,0:T(4,128)(2,1)S(1)}, bf16[4,400]{1,0:T(4,128)(2,1)S(1)}, u32[]{:S(2)}, u32[]{:S(2)}) collective-permute-start(bf16[4,400]{1,0:T(4,128)(2,1)S(1)} %pad_maximum_fusion.13.refs_0_), channel_id=1, source_target_pairs={{0,64},{16,80},{32,96},{48,112},{64,0},{80,16},{96,32},{112,48},{1... | collective-permute-start | bytes 9608 | tf_op jit(solution)/shard_map/while/body/eval_jaxpr/ppermute | solution.py:323
  16.0 3.6 %collective-permute-start.2 = (bf16[4,400]{1,0:T(4,128)(2,1)S(1)}, bf16[4,400]{1,0:T(4,128)(2,1)S(1)}, u32[]{:S(2)}, u32[]{:S(2)}) collective-permute-start(bf16[4,400]{1,0:T(4,128)(2,1)S(1)} %pad_maximum_fusion.13.refs_0_), channel_id=1, source_target_pairs={{0,96},{16,112},{32,0},{48,16},{64,32},{80,48},{96,64},{112,80},{1... | collective-permute-start | bytes 9608 | tf_op jit(solution)/shard_map/while/body/eval_jaxpr/ppermute | solution.py:323
  22.7 2.7 %collective-permute-start.5 = (f32[2,960,128]{2,1,0:T(8,128)S(1)}, f32[2,960,128]{2,1,0:T(8,128)S(1)}, u32[]{:S(2)}, u32[]{:S(2)}) collective-permute-start(f32[2,960,128]{2,1,0:T(8,128)S(1)} %get-tuple-element.218), channel_id=1, source_target_pairs={{0,16},{16,0},{32,48},{48,32},{64,80},{80,64},{96,112},{112,96},{1... | collective-permute-start | bytes 2949128 | tf_op jit(solution)/shard_map/while/body/eval_jaxpr/ppermute | solution.py:317
  24.3 8.2 %collective-permute-start.10 = (f32[2,960,128]{2,1,0:T(8,128)S(1)}, f32[2,960,128]{2,1,0:T(8,128)S(1)}, u32[]{:S(2)}, u32[]{:S(2)}) collective-permute-start(f32[2,960,128]{2,1,0:T(8,128)S(1)} %get-tuple-element.228), channel_id=1, source_target_pairs={{0,16},{16,0},{32,48},{48,32},{64,80},{80,64},{96,112},{112,96},{1... | collective-permute-start | bytes 2949128 | tf_op jit(solution)/shard_map/while/body/eval_jaxpr/ppermute | solution.py:317
  25.4 9.3 %collective-permute-start.11 = (bf16[960,128]{1,0:T(8,128)(2,1)S(1)}, bf16[960,128]{1,0:T(8,128)(2,1)S(1)}, u32[]{:S(2)}, u32[]{:S(2)}) collective-permute-start(bf16[960,128]{1,0:T(8,128)(2,1)S(1)} %get-tuple-element.220), channel_id=1, source_target_pairs={{0,32},{16,48},{32,64},{48,80},{64,96},{80,112},{96,0},{112,16},{1... | collective-permute-start | bytes 737288 | tf_op jit(solution)/shard_map/while/body/eval_jaxpr/ppermute | solution.py:323
  25.7 9.3 %collective-permute-start.8 = (bf16[960,128]{1,0:T(8,128)(2,1)S(1)}, bf16[960,128]{1,0:T(8,128)(2,1)S(1)}, u32[]{:S(2)}, u32[]{:S(2)}) collective-permute-start(bf16[960,128]{1,0:T(8,128)(2,1)S(1)} %get-tuple-element.221), channel_id=1, source_target_pairs={{0,96},{16,112},{32,0},{48,16},{64,32},{80,48},{96,64},{112,80},{1... | collective-permute-start | bytes 737288 | tf_op jit(solution)/shard_map/while/body/eval_jaxpr/ppermute | solution.py:323
  30.2 24.4 %copy-start.5 = (f32[1,400]{1,0:T(1,128)S(1)}, f32[1,400]{1,0:T(1,128)}, u32[]{:S(2)}) copy-start(f32[1,400]{1,0:T(1,128)} %get-tuple-element.275.prec_ref) | copy-start | bytes 4804 | tf_op jit(solution)/shard_map/while
  30.2 24.4 %copy-start.6 = (f32[300]{0:T(512)S(1)}, f32[300]{0:T(512)}, u32[]{:S(2)}) copy-start(f32[300]{0:T(512)} %get-tuple-element.276.weight_ref) | copy-start | bytes 3604 | tf_op jit(solution)/shard_map/while
  30.2 4.7 %collective-permute-start.7 = (f32[2,960,128]{2,1,0:T(8,128)S(1)}, f32[2,960,128]{2,1,0:T(8,128)S(1)}, u32[]{:S(2)}, u32[]{:S(2)}) collective-permute-start(f32[2,960,128]{2,1,0:T(8,128)S(1)} %get-tuple-element.227), channel_id=1, source_target_pairs={{0,16},{16,0},{32,48},{48,32},{64,80},{80,64},{96,112},{112,96},{1... | collective-permute-start | bytes 2949128 | tf_op jit(solution)/shard_map/while/body/eval_jaxpr/ppermute | solution.py:317
  31.8 28.1 %copy-start.7 = (f32[1,400]{1,0:T(1,128)S(1)}, f32[1,400]{1,0:T(1,128)}, u32[]{:S(2)}) copy-start(f32[1,400]{1,0:T(1,128)} %get-tuple-element.277.mean_ref) | copy-start | bytes 4804 | tf_op jit(solution)/shard_map/while
  31.9 11.9 %collective-permute-start.6 = (f32[2,960,128]{2,1,0:T(8,128)S(1)}, f32[2,960,128]{2,1,0:T(8,128)S(1)}, u32[]{:S(2)}, u32[]{:S(2)}) collective-permute-start(f32[2,960,128]{2,1,0:T(8,128)S(1)} %get-tuple-element.225), channel_id=1, source_target_pairs={{0,16},{16,0},{32,48},{48,32},{64,80},{80,64},{96,112},{112,96},{1... | collective-permute-start | bytes 2949128 | tf_op jit(solution)/shard_map/while/body/eval_jaxpr/ppermute | solution.py:317
  34.8 9.0 %collective-permute-start.15 = (bf16[2,400,128]{2,1,0:T(8,128)(2,1)S(1)}, bf16[2,400,128]{2,1,0:T(8,128)(2,1)S(1)}, u32[]{:S(2)}, u32[]{:S(2)}) collective-permute-start(bf16[2,400,128]{2,1,0:T(8,128)(2,1)S(1)} %pad_maximum_fusion.17), channel_id=1, source_target_pairs={{0,32},{16,48},{32,64},{48,80},{64,96},{80,112},{96,0},{112,16},{1... | collective-permute-start | bytes 614408 | tf_op jit(solution)/shard_map/while/body/eval_jaxpr/ppermute | solution.py:323
  35.1 8.7 %collective-permute-start.14 = (bf16[2,400,128]{2,1,0:T(8,128)(2,1)S(1)}, bf16[2,400,128]{2,1,0:T(8,128)(2,1)S(1)}, u32[]{:S(2)}, u32[]{:S(2)}) collective-permute-start(bf16[2,400,128]{2,1,0:T(8,128)(2,1)S(1)} %pad_maximum_fusion.16), channel_id=1, source_target_pairs={{0,96},{16,112},{32,0},{48,16},{64,32},{80,48},{96,64},{112,80},{1... | collective-permute-start | bytes 614408 | tf_op jit(solution)/shard_map/while/body/eval_jaxpr/ppermute | solution.py:323
  38.4 11.5 %collective-permute-start.12 = (bf16[2,560,128]{2,1,0:T(8,128)(2,1)S(1)}, bf16[2,560,128]{2,1,0:T(8,128)(2,1)S(1)}, u32[]{:S(2)}, u32[]{:S(2)}) collective-permute-start(bf16[2,560,128]{2,1,0:T(8,128)(2,1)S(1)} %pad_maximum_fusion.15), channel_id=1, source_target_pairs={{0,32},{16,48},{32,64},{48,80},{64,96},{80,112},{96,0},{112,16},{1... | collective-permute-start | bytes 860168 | tf_op jit(solution)/shard_map/while/body/eval_jaxpr/ppermute | solution.py:323
  38.5 11.4 %collective-permute-start.9 = (bf16[2,560,128]{2,1,0:T(8,128)(2,1)S(1)}, bf16[2,560,128]{2,1,0:T(8,128)(2,1)S(1)}, u32[]{:S(2)}, u32[]{:S(2)}) collective-permute-start(bf16[2,560,128]{2,1,0:T(8,128)(2,1)S(1)} %pad_maximum_fusion.14), channel_id=1, source_target_pairs={{0,96},{16,112},{32,0},{48,16},{64,32},{80,48},{96,64},{112,80},{1... | collective-permute-start | bytes 860168 | tf_op jit(solution)/shard_map/while/body/eval_jaxpr/ppermute | solution.py:323
  43.8 10.7 %collective-permute-start.16 = (bf16[400,128]{1,0:T(8,128)(2,1)S(1)}, bf16[400,128]{1,0:T(8,128)(2,1)S(1)}, u32[]{:S(2)}, u32[]{:S(2)}) collective-permute-start(bf16[400,128]{1,0:T(8,128)(2,1)S(1)} %get-tuple-element.235), channel_id=1, source_target_pairs={{0,128},{16,144},{32,160},{48,176},{64,192},{80,208},{96,224},{112... | collective-permute-start | bytes 307208 | tf_op jit(solution)/shard_map/while/body/eval_jaxpr/ppermute | solution.py:329
  50.0 9.9 %collective-permute-start.13 = (bf16[560,128]{1,0:T(8,128)(2,1)S(1)}, bf16[560,128]{1,0:T(8,128)(2,1)S(1)}, u32[]{:S(2)}, u32[]{:S(2)}) collective-permute-start(bf16[560,128]{1,0:T(8,128)(2,1)S(1)} %get-tuple-element.232), channel_id=1, source_target_pairs={{0,128},{16,144},{32,160},{48,176},{64,192},{80,208},{96,224},{112... | collective-permute-start | bytes 430088 | tf_op jit(solution)/shard_map/while/body/eval_jaxpr/ppermute | solution.py:329
  67.2 1.2 collective-permute-start
  68.5 7.6 %collective-permute-start.1 = (bf16[2,400]{1,0:T(2,128)(2,1)S(1)}, bf16[2,400]{1,0:T(2,128)(2,1)S(1)}, u32[]{:S(2)}, u32[]{:S(2)}) collective-permute-start(bf16[2,400]{1,0:T(2,128)(2,1)S(1)} %pad_maximum_fusion.12), channel_id=1, source_target_pairs={{0,128},{16,144},{32,160},{48,176},{64,192},{80,208},{96,224},{112... | collective-permute-start | bytes 4808 | tf_op jit(solution)/shard_map/while/body/eval_jaxpr/ppermute | solution.py:329
  76.1 8.6 %slice-start = ((s8[8192000]{0:T(1024)(128)(4,1)}), s8[4194304]{0:T(1024)(128)(4,1)S(1)}, s32[]{:S(2)}) async-start(s8[8192000]{0:T(1024)(128)(4,1)} %bitcast.79), calls=%async_computation | async-start | bytes 8388608 | tf_op jit(solution)/shard_map/while
  76.1 8.6 %slice-start.1 = ((s8[8192000]{0:T(1024)(128)(4,1)}), s8[3997696]{0:T(1024)(128)(4,1)S(1)}, s32[]{:S(2)}) async-start(s8[8192000]{0:T(1024)(128)(4,1)} %bitcast.79), calls=%async_computation.1 | async-start | bytes 7995392 | tf_op jit(solution)/shard_map/while
  76.1 8.5 %copy-start = (bf16[300,528]{1,0:T(8,128)(2,1)S(1)}, bf16[300,528]{1,0:T(8,128)(2,1)}, u32[]{:S(2)}) copy-start(bf16[300,528]{1,0:T(8,128)(2,1)} %get-tuple-element.273.refs_8_.eig_ref) | copy-start | bytes 950404 | tf_op jit(solution)/shard_map/while
  76.1 8.5 %copy-start.1 = (bf16[16,528]{1,0:T(8,128)(2,1)S(1)}, bf16[16,528]{1,0:T(8,128)(2,1)}, u32[]{:S(2)}) copy-start(bf16[16,528]{1,0:T(8,128)(2,1)} %get-tuple-element.270.refs_4_) | copy-start | bytes 50692 | tf_op jit(solution)/shard_map/while
  76.1 8.5 %copy-start.2 = (bf16[528]{0:T(1024)(128)(2,1)S(1)}, bf16[528]{0:T(1024)(128)(2,1)}, u32[]{:S(2)}) copy-start(bf16[528]{0:T(1024)(128)(2,1)} %get-tuple-element.271.refs_6_) | copy-start | bytes 3172 | tf_op jit(solution)/shard_map/while
  76.1 8.5 %copy-start.3 = (bf16[528]{0:T(1024)(128)(2,1)S(1)}, bf16[528]{0:T(1024)(128)(2,1)}, u32[]{:S(2)}) copy-start(bf16[528]{0:T(1024)(128)(2,1)} %get-tuple-element.272.refs_7_) | copy-start | bytes 3172 | tf_op jit(solution)/shard_map/while
  76.1 5.7 %collective-permute-start.4 = (bf16[4,400]{1,0:T(4,128)(2,1)S(1)}, bf16[4,400]{1,0:T(4,128)(2,1)S(1)}, u32[]{:S(2)}, u32[]{:S(2)}) collective-permute-start(bf16[4,400]{1,0:T(4,128)(2,1)S(1)} %pad_maximum_fusion.13.refs_0_), channel_id=1, source_target_pairs={{0,32},{16,48},{32,64},{48,80},{64,96},{80,112},{96,0},{112,16},{1... | collective-permute-start | bytes 9608 | tf_op jit(solution)/shard_map/while/body/eval_jaxpr/ppermute | solution.py:323
  76.2 6.4 %collective-permute-start.3 = (bf16[4,400]{1,0:T(4,128)(2,1)S(1)}, bf16[4,400]{1,0:T(4,128)(2,1)S(1)}, u32[]{:S(2)}, u32[]{:S(2)}) collective-permute-start(bf16[4,400]{1,0:T(4,128)(2,1)S(1)} %pad_maximum_fusion.13.refs_0_), channel_id=1, source_target_pairs={{0,64},{16,80},{32,96},{48,112},{64,0},{80,16},{96,32},{112,48},{1... | collective-permute-start | bytes 9608 | tf_op jit(solution)/shard_map/while/body/eval_jaxpr/ppermute | solution.py:323
  81.0 3.6 %collective-permute-start.2 = (bf16[4,400]{1,0:T(4,128)(2,1)S(1)}, bf16[4,400]{1,0:T(4,128)(2,1)S(1)}, u32[]{:S(2)}, u32[]{:S(2)}) collective-permute-start(bf16[4,400]{1,0:T(4,128)(2,1)S(1)} %pad_maximum_fusion.13.refs_0_), channel_id=1, source_target_pairs={{0,96},{16,112},{32,0},{48,16},{64,32},{80,48},{96,64},{112,80},{1... | collective-permute-start | bytes 9608 | tf_op jit(solution)/shard_map/while/body/eval_jaxpr/ppermute | solution.py:323
  87.7 2.7 %collective-permute-start.5 = (f32[2,960,128]{2,1,0:T(8,128)S(1)}, f32[2,960,128]{2,1,0:T(8,128)S(1)}, u32[]{:S(2)}, u32[]{:S(2)}) collective-permute-start(f32[2,960,128]{2,1,0:T(8,128)S(1)} %get-tuple-element.218), channel_id=1, source_target_pairs={{0,16},{16,0},{32,48},{48,32},{64,80},{80,64},{96,112},{112,96},{1... | collective-permute-start | bytes 2949128 | tf_op jit(solution)/shard_map/while/body/eval_jaxpr/ppermute | solution.py:317
  89.3 8.2 %collective-permute-start.10 = (f32[2,960,128]{2,1,0:T(8,128)S(1)}, f32[2,960,128]{2,1,0:T(8,128)S(1)}, u32[]{:S(2)}, u32[]{:S(2)}) collective-permute-start(f32[2,960,128]{2,1,0:T(8,128)S(1)} %get-tuple-element.228), channel_id=1, source_target_pairs={{0,16},{16,0},{32,48},{48,32},{64,80},{80,64},{96,112},{112,96},{1... | collective-permute-start | bytes 2949128 | tf_op jit(solution)/shard_map/while/body/eval_jaxpr/ppermute | solution.py:317
  90.4 9.3 %collective-permute-start.11 = (bf16[960,128]{1,0:T(8,128)(2,1)S(1)}, bf16[960,128]{1,0:T(8,128)(2,1)S(1)}, u32[]{:S(2)}, u32[]{:S(2)}) collective-permute-start(bf16[960,128]{1,0:T(8,128)(2,1)S(1)} %get-tuple-element.220), channel_id=1, source_target_pairs={{0,32},{16,48},{32,64},{48,80},{64,96},{80,112},{96,0},{112,16},{1... | collective-permute-start | bytes 737288 | tf_op jit(solution)/shard_map/while/body/eval_jaxpr/ppermute | solution.py:323
  90.5 9.4 %collective-permute-start.8 = (bf16[960,128]{1,0:T(8,128)(2,1)S(1)}, bf16[960,128]{1,0:T(8,128)(2,1)S(1)}, u32[]{:S(2)}, u32[]{:S(2)}) collective-permute-start(bf16[960,128]{1,0:T(8,128)(2,1)S(1)} %get-tuple-element.221), channel_id=1, source_target_pairs={{0,96},{16,112},{32,0},{48,16},{64,32},{80,48},{96,64},{112,80},{1... | collective-permute-start | bytes 737288 | tf_op jit(solution)/shard_map/while/body/eval_jaxpr/ppermute | solution.py:323
  95.2 23.8 %copy-start.5 = (f32[1,400]{1,0:T(1,128)S(1)}, f32[1,400]{1,0:T(1,128)}, u32[]{:S(2)}) copy-start(f32[1,400]{1,0:T(1,128)} %get-tuple-element.275.prec_ref) | copy-start | bytes 4804 | tf_op jit(solution)/shard_map/while
  95.2 23.7 %copy-start.6 = (f32[300]{0:T(512)S(1)}, f32[300]{0:T(512)}, u32[]{:S(2)}) copy-start(f32[300]{0:T(512)} %get-tuple-element.276.weight_ref) | copy-start | bytes 3604 | tf_op jit(solution)/shard_map/while
  95.2 4.7 %collective-permute-start.7 = (f32[2,960,128]{2,1,0:T(8,128)S(1)}, f32[2,960,128]{2,1,0:T(8,128)S(1)}, u32[]{:S(2)}, u32[]{:S(2)}) collective-permute-start(f32[2,960,128]{2,1,0:T(8,128)S(1)} %get-tuple-element.227), channel_id=1, source_target_pairs={{0,16},{16,0},{32,48},{48,32},{64,80},{80,64},{96,112},{112,96},{1... | collective-permute-start | bytes 2949128 | tf_op jit(solution)/shard_map/while/body/eval_jaxpr/ppermute | solution.py:317
  96.8 27.8 %copy-start.7 = (f32[1,400]{1,0:T(1,128)S(1)}, f32[1,400]{1,0:T(1,128)}, u32[]{:S(2)}) copy-start(f32[1,400]{1,0:T(1,128)} %get-tuple-element.277.mean_ref) | copy-start | bytes 4804 | tf_op jit(solution)/shard_map/while
  96.8 11.9 %collective-permute-start.6 = (f32[2,960,128]{2,1,0:T(8,128)S(1)}, f32[2,960,128]{2,1,0:T(8,128)S(1)}, u32[]{:S(2)}, u32[]{:S(2)}) collective-permute-start(f32[2,960,128]{2,1,0:T(8,128)S(1)} %get-tuple-element.225), channel_id=1, source_target_pairs={{0,16},{16,0},{32,48},{48,32},{64,80},{80,64},{96,112},{112,96},{1... | collective-permute-start | bytes 2949128 | tf_op jit(solution)/shard_map/while/body/eval_jaxpr/ppermute | solution.py:317
  99.8 9.0 %collective-permute-start.15 = (bf16[2,400,128]{2,1,0:T(8,128)(2,1)S(1)}, bf16[2,400,128]{2,1,0:T(8,128)(2,1)S(1)}, u32[]{:S(2)}, u32[]{:S(2)}) collective-permute-start(bf16[2,400,128]{2,1,0:T(8,128)(2,1)S(1)} %pad_maximum_fusion.17), channel_id=1, source_target_pairs={{0,32},{16,48},{32,64},{48,80},{64,96},{80,112},{96,0},{112,16},{1... | collective-permute-start | bytes 614408 | tf_op jit(solution)/shard_map/while/body/eval_jaxpr/ppermute | solution.py:323
  100.1 8.7 %collective-permute-start.14 = (bf16[2,400,128]{2,1,0:T(8,128)(2,1)S(1)}, bf16[2,400,128]{2,1,0:T(8,128)(2,1)S(1)}, u32[]{:S(2)}, u32[]{:S(2)}) collective-permute-start(bf16[2,400,128]{2,1,0:T(8,128)(2,1)S(1)} %pad_maximum_fusion.16), channel_id=1, source_target_pairs={{0,96},{16,112},{32,0},{48,16},{64,32},{80,48},{96,64},{112,80},{1... | collective-permute-start | bytes 614408 | tf_op jit(solution)/shard_map/while/body/eval_jaxpr/ppermute | solution.py:323
  103.4 10.9 %collective-permute-start.12 = (bf16[2,560,128]{2,1,0:T(8,128)(2,1)S(1)}, bf16[2,560,128]{2,1,0:T(8,128)(2,1)S(1)}, u32[]{:S(2)}, u32[]{:S(2)}) collective-permute-start(bf16[2,560,128]{2,1,0:T(8,128)(2,1)S(1)} %pad_maximum_fusion.15), channel_id=1, source_target_pairs={{0,32},{16,48},{32,64},{48,80},{64,96},{80,112},{96,0},{112,16},{1... | collective-permute-start | bytes 860168 | tf_op jit(solution)/shard_map/while/body/eval_jaxpr/ppermute | solution.py:323
  103.5 10.8 %collective-permute-start.9 = (bf16[2,560,128]{2,1,0:T(8,128)(2,1)S(1)}, bf16[2,560,128]{2,1,0:T(8,128)(2,1)S(1)}, u32[]{:S(2)}, u32[]{:S(2)}) collective-permute-start(bf16[2,560,128]{2,1,0:T(8,128)(2,1)S(1)} %pad_maximum_fusion.14), channel_id=1, source_target_pairs={{0,96},{16,112},{32,0},{48,16},{64,32},{80,48},{96,64},{112,80},{1... | collective-permute-start | bytes 860168 | tf_op jit(solution)/shard_map/while/body/eval_jaxpr/ppermute | solution.py:323
  108.8 10.1 %collective-permute-start.16 = (bf16[400,128]{1,0:T(8,128)(2,1)S(1)}, bf16[400,128]{1,0:T(8,128)(2,1)S(1)}, u32[]{:S(2)}, u32[]{:S(2)}) collective-permute-start(bf16[400,128]{1,0:T(8,128)(2,1)S(1)} %get-tuple-element.235), channel_id=1, source_target_pairs={{0,128},{16,144},{32,160},{48,176},{64,192},{80,208},{96,224},{112... | collective-permute-start | bytes 307208 | tf_op jit(solution)/shard_map/while/body/eval_jaxpr/ppermute | solution.py:329
  114.3 10.3 %collective-permute-start.13 = (bf16[560,128]{1,0:T(8,128)(2,1)S(1)}, bf16[560,128]{1,0:T(8,128)(2,1)S(1)}, u32[]{:S(2)}, u32[]{:S(2)}) collective-permute-start(bf16[560,128]{1,0:T(8,128)(2,1)S(1)} %get-tuple-element.232), channel_id=1, source_target_pairs={{0,128},{16,144},{32,160},{48,176},{64,192},{80,208},{96,224},{112... | collective-permute-start | bytes 430088 | tf_op jit(solution)/shard_map/while/body/eval_jaxpr/ppermute | solution.py:329
  (5 other events, 33.4 us)
